TPU v7x, 256 devices: a 2x2x32 block of a 4x8x32 slice. The times are simulated.
256 devices in a mesh: groups: 4 (over y, x), sph: 64 (over z, core).
Axes of the slice: x: 2, y: 2, z: 32, core: 2. Of those that a mesh axis runs over, the one named last changes fastest.
The devices are a block of a 4x8x32 slice.
Arguments:
- positions: float32 [2048, 3], P('sph'), may hold values from -8 to 8
- wave_vectors: float32 [256, 3], replicated, may hold values from -5 to 5
- pattern: float32 [2, 448, 256], replicated, may hold values from -6 to 6
- dir_index: int32 [128], P('groups'), parts along dimension 0, may hold values from 0 to 255
- mie: float32 [2, 448, 2048], P(None, None, 'sph'), may hold values from -0.9 to 0.9
- trans_table: bfloat16 [8, 2, 448, 448], replicated, may hold values from -0.1875 to 0.1875
- pair_route: int32 [4096, 1], P('sph'), may hold values from 0 to 63; in each aligned block of 64 rows (0 to 63, 64 to 127, ...) at most 2 rows name the same one
- pair_source: int32 [4096], P('sph'), may hold values from 0 to 15
- pair_target: int32 [4096], P('sph'), may hold values from 0 to 15
- pair_class: int32 [4096], P('sph'), may hold values from 0 to 7
Outputs:
- scattered: bfloat16 [896, 262144], P(None, ('groups', 'sph')), parts along dimension 1
- extinction: float32 [128], P('groups'), parts along dimension 0
There are 4 independent parts, one for each index of `groups`. A program takes and returns all parts, laid end to end along the dimension named above; an argument that names none is the same for every part. Nothing has to cross between parts.
Inputs may be any that keep to these rules, and one draw needn't show every extreme that they name: `pair_route`: among the rows of one device no device is named by more than 2 pairs, and in every draw some device is named by exactly 2 of them.
All inputs are finite; a program needn't handle non-finite values.
Results may differ from a plain program's by a relative error of at most 0.0051.
Values may be sent and summed in bfloat16 or wider, within the bound.
A program may use at most 192 MiB of HBM per device.

v0:
```python
import jax
import jax.numpy as jnp
from jax import lax
from jax.sharding import PartitionSpec as P

BLOCK = 2


HIGHEST_PRECISION = lax.Precision.HIGHEST


def sent_to_all(x, axis):
    copies = jnp.broadcast_to(x, (lax.axis_size(axis), *x.shape))
    return lax.all_to_all(copies, axis, split_axis=0, concat_axis=0, tiled=True)


def taken_together(x, axis):
    return sent_to_all(x, axis).sum(axis=0)


def incident_field(positions, wave_vectors, pattern, dir_index):
    table_rows = wave_vectors.shape[0]
    select = (jnp.arange(table_rows, dtype=jnp.int32)[:, None] == dir_index[None, :]).astype(
        jnp.float32
    )
    directions = jnp.dot(select.T, wave_vectors, precision=HIGHEST_PRECISION)
    phases = (
        positions[:, 0:1] * directions[None, :, 0]
        + positions[:, 1:2] * directions[None, :, 1]
        + positions[:, 2:3] * directions[None, :, 2]
    )
    cosine = jnp.cos(phases)
    sine_part = jnp.sin(phases)
    chosen = jnp.einsum("cmt,td->cmd", pattern, select, precision=HIGHEST_PRECISION)
    inc_real = cosine[None] * chosen[0][:, None, :] - sine_part[None] * chosen[1][:, None, :]
    inc_imag = cosine[None] * chosen[1][:, None, :] + sine_part[None] * chosen[0][:, None, :]
    return (inc_real, inc_imag)


def translate(trans_table, classes, block_values):
    item_count = classes.shape[0]
    mode_count = trans_table.shape[2]
    grouped_classes = classes.reshape(item_count // 8, 8)
    grouped_values = block_values.reshape((item_count // 8, 8) + block_values.shape[1:])

    def one_group(group_items):
        picked, values = group_items
        tables = trans_table[picked]
        data_real = values[:, :mode_count]
        data_imag = values[:, mode_count:]
        part_real = jnp.einsum(
            "kij,kjc->kic", tables[:, 0], data_real, preferred_element_type=jnp.float32
        ) - jnp.einsum("kij,kjc->kic", tables[:, 1], data_imag, preferred_element_type=jnp.float32)
        part_imag = jnp.einsum(
            "kij,kjc->kic", tables[:, 1], data_real, preferred_element_type=jnp.float32
        ) + jnp.einsum("kij,kjc->kic", tables[:, 0], data_imag, preferred_element_type=jnp.float32)
        return jnp.concatenate([part_real, part_imag], 1).astype(jnp.bfloat16)

    return lax.map(one_group, (grouped_classes, grouped_values)).reshape(block_values.shape)


def shards(
    positions,
    wave_vectors,
    pattern,
    dir_index,
    mie,
    trans_table,
    pair_route,
    pair_source,
    pair_target,
    pair_class,
):
    mode_count = pattern.shape[1]
    spheres = positions.shape[0]
    directions = dir_index.shape[0]
    columns = BLOCK * directions
    block_count = spheres // BLOCK
    devices = lax.axis_size("sph")
    pair_count = pair_source.shape[0]
    capacity = max(2, 2 * pair_count // devices)
    slot_count = devices * capacity
    inc_real, inc_imag = incident_field(positions, wave_vectors, pattern, dir_index)
    mie_real = mie[0][:, :, None]
    mie_imag = mie[1][:, :, None]
    scat_real = mie_real * inc_real - mie_imag * inc_imag
    scat_imag = mie_real * inc_imag + mie_imag * inc_real
    coeffs = jnp.concatenate([scat_real, scat_imag], 0).astype(jnp.bfloat16)
    block_data = coeffs.reshape(2 * mode_count, block_count, columns).transpose(1, 0, 2)
    dest_device = pair_route[:, 0]
    by_device = (dest_device[:, None] == jnp.arange(devices, dtype=jnp.int32)[None, :]).astype(
        jnp.int32
    )
    before = jnp.cumsum(by_device, axis=0) - by_device
    rank_in = jnp.sum(before * by_device, axis=1)
    slot_of = dest_device * capacity + rank_in
    slot_match = (jnp.arange(slot_count, dtype=jnp.int32)[:, None] == slot_of[None, :]).astype(
        jnp.int32
    )
    filled = jnp.sum(slot_match, axis=1)
    slot_pair = jnp.sum(slot_match * jnp.arange(pair_count, dtype=jnp.int32)[None, :], axis=1)
    slot_target = jnp.where(filled > 0, pair_target[slot_pair], -1)
    keep_slot = filled.astype(jnp.bfloat16)[:, None, None]
    computed = translate(trans_table, pair_class, block_data[pair_source])
    outgoing = computed[slot_pair] * keep_slot
    outgoing = outgoing.reshape(devices, capacity, 2 * mode_count, columns)
    arrived = lax.all_to_all(outgoing, "sph", split_axis=0, concat_axis=0, tiled=True)
    targets = lax.all_to_all(
        slot_target.reshape(devices, capacity), "sph", split_axis=0, concat_axis=0, tiled=True
    ).reshape(slot_count)
    partial_value = arrived.reshape(slot_count, 2 * mode_count, columns)
    gather_matrix = (jnp.arange(block_count, dtype=jnp.int32)[:, None] == targets[None, :]).astype(
        jnp.bfloat16
    )
    summed = jnp.dot(
        gather_matrix,
        partial_value.reshape(slot_count, 2 * mode_count * columns),
        preferred_element_type=jnp.float32,
    )
    summed = (
        summed.reshape(block_count, 2 * mode_count, columns)
        .transpose(1, 0, 2)
        .reshape(2 * mode_count, spheres, directions)
    )
    total_real = inc_real + summed[:mode_count]
    total_imag = inc_imag + summed[mode_count:]
    out_real = mie_real * total_real - mie_imag * total_imag
    out_imag = mie_real * total_imag + mie_imag * total_real
    scattered = (
        jnp.concatenate([out_real, out_imag], 0)
        .reshape(2 * mode_count, spheres * directions)
        .astype(jnp.bfloat16)
    )
    local_ext = jnp.sum(inc_real * out_real + inc_imag * out_imag, axis=(0, 1))
    extinction = taken_together(local_ext, "sph")
    return (scattered, extinction)


def solution(mesh):
    placed = (
        P("sph", None),
        P(),
        P(),
        P("groups"),
        P(None, None, "sph"),
        P(),
        P("sph", None),
        P("sph"),
        P("sph"),
        P("sph"),
    )
    return jax.shard_map(
        shards,
        mesh=mesh,
        in_specs=placed,
        out_specs=(P(None, ("groups", "sph")), P("groups")),
        check_vma=False,
    )
```

profile of v0, /device:TPU:37, one launch (start us, length us, event | category | flops | bytes accessed | tf_op | source)
XLA Modules:
  0.0 1669.5 jit_solution(18412838379045699855)
XLA Ops:
  5.6 34.9 %all-to-all-start = ((s32[64,1,2]{2,1,0:T(1,128)}), s32[64,1,2]{2,1,0:T(1,128)S(1)}, u32[]{:S(2)}, u32[]{:S(2)}) async-start(s32[64,1,2]{2,1,0:T(1,128)} %bitcast.24), calls=%async_computation | async-start | bytes 65536 | tf_op jit(solution)/shard_map/all_to_all | solution.py:108
  49.5 4.3 gather_fusion.2
  53.8 134.5 %while.10 = (s32[]{:T(128)}, bf16[8,8,896,64]{2,3,1,0:T(8,128)(2,1)}, s32[8,8]{1,0:T(8,128)S(1)}, bf16[8,2,448,448]{3,2,1,0:T(8,128)(2,1)}, bf16[8,8,896,64]{2,3,1,0:T(8,128)(2,1)}, /*index=5*/s32[]{:T(128)}) while((s32[]{:T(128)}, bf16[8,8,896,64]{2,3,1,0:T(8,128)(2,1)}, s32[8,8]{1,0:T(8,128)S(1)}, bf16[8,2,448,448]{3,2,1,0:T(8,128)(2,1)}, ...), condition=%wide.region_5.6_spmd, body=%wide.region_4.5_spmd.sunk | while | flops 824837120 | bytes 63836904 | solution.py:59
  53.8 7.0 gather_fusion
  70.6 7.0 gather_fusion
  87.5 7.0 gather_fusion
  95.9 3.5 fusion.68
  104.3 7.0 gather_fusion
  121.1 7.0 gather_fusion
  137.9 7.0 gather_fusion
  154.7 7.0 gather_fusion
  163.1 3.5 fusion.68
  171.6 7.0 gather_fusion
  188.4 12.2 gather_fusion.3
  200.8 13.5 broadcast_multiply_fusion
  214.3 23.3 %all-to-all-start.1 = ((bf16[64,2,896,64]{2,3,1,0:T(8,128)(2,1)}), bf16[64,2,896,64]{2,3,1,0:T(8,128)(2,1)}, u32[]{:S(2)}, u32[]{:S(2)}) async-start(bf16[64,2,896,64]{2,3,1,0:T(8,128)(2,1)} %broadcast_multiply_fusion), calls=%async_computation.1 | async-start | bytes 29360128 | tf_op jit(solution)/shard_map/all_to_all | solution.py:107
  239.7 1253.7 %all-to-all-done.1 = bf16[64,2,896,64]{2,3,1,0:T(8,128)(2,1)} async-done(((bf16[64,2,896,64]{2,3,1,0:T(8,128)(2,1)}), bf16[64,2,896,64]{2,3,1,0:T(8,128)(2,1)}, u32[]{:S(2)}, u32[]{:S(2)}) %all-to-all-start.1) | async-done | bytes 14680096 | tf_op jit(solution)/shard_map/all_to_all | solution.py:107
  1493.4 26.5 %copy.100 = bf16[64,2,896,64]{3,2,1,0:T(8,128)(2,1)} copy(bf16[64,2,896,64]{2,3,1,0:T(8,128)(2,1)} %all-to-all-done.1) | data formatting | bytes 29360128 | tf_op jit(solution)/shard_map/all_to_all | solution.py:107
  1519.9 28.1 %reshape_reshape.3 = bf16[128,57344]{1,0:T(8,128)(2,1)} reshape(bf16[64,2,896,64]{3,2,1,0:T(8,128)(2,1)} %copy.100) | data formatting | bytes 29360128 | tf_op jit(solution)/shard_map/reshape;reshape | solution.py:117
  1548.1 20.2 %copy.101 = bf16[57344,128]{1,0:T(8,128)(2,1)} copy(bf16[57344,128]{0,1:T(8,128)(2,1)} %bitcast.238) | data formatting | bytes 29360128 | tf_op jit(solution)/shard_map/dot_general | solution.py:115
  1568.3 35.5 %fusion.34 = f32[896,16,64]{0,1,2:T(8,128)} fusion(bf16[896,64,128]{2,1,0:T(8,128)(2,1)} %bitcast.237, s32[128]{0:T(128)S(1)} %eq.64), kind=kOutput, calls=%fused_computation.61 | convolution fusion | flops 234883072 | bytes 18350592 | tf_op jit(solution)/shard_map/dot_general | solution.py:115
  1603.8 10.2 add_reduce_fusion
  1618.6 27.9 %all-to-all-start.2 = ((f32[64,1,32]{2,1,0:T(1,128)}), f32[64,1,32]{2,1,0:T(1,128)S(1)}, u32[]{:S(2)}, u32[]{:S(2)}) async-start(f32[64,1,32]{2,1,0:T(1,128)} %broadcast_in_dim.14), calls=%async_computation.2 | async-start | bytes 65536 | tf_op jit(solution)/shard_map/all_to_all | solution.py:14
  1652.1 16.6 all-to-all-done.2
  (195 shorter events, 97.9 us)
Async XLA Ops:
  0.6 43.2 %copy-start = (f32[2,448,256]{2,1,0:T(8,128)S(1)}, f32[2,448,256]{2,1,0:T(8,128)}, u32[]{:S(2)}) copy-start(f32[2,448,256]{2,1,0:T(8,128)} %param.14) | copy-start | bytes 2752516
  0.6 44.4 %copy-start.20 = (s32[64]{0:T(128)S(1)}, s32[64]{0:T(128)}, u32[]{:S(2)}) copy-start(s32[64]{0:T(128)} %param.19) | copy-start | bytes 772
  0.7 44.4 %copy-start.19 = (s32[64]{0:T(128)S(1)}, s32[64]{0:T(128)}, u32[]{:S(2)}) copy-start(s32[64]{0:T(128)} %param.21) | copy-start | bytes 772
  0.7 44.5 %copy-start.18 = (f32[2,448,32]{1,2,0:T(8,128)S(1)}, f32[2,448,32]{1,2,0:T(8,128)}, u32[]{:S(2)}) copy-start(f32[2,448,32]{1,2,0:T(8,128)} %param.16) | copy-start | bytes 344068
  5.6 208.7 %all-to-all-start = ((s32[64,1,2]{2,1,0:T(1,128)}), s32[64,1,2]{2,1,0:T(1,128)S(1)}, u32[]{:S(2)}, u32[]{:S(2)}) async-start(s32[64,1,2]{2,1,0:T(1,128)} %bitcast.24), calls=%async_computation | async-start | bytes 65536 | tf_op jit(solution)/shard_map/all_to_all | solution.py:108
  46.4 2.5 copy-start.9
  60.9 4.9 copy-start.2
  77.7 4.9 copy-start.2
  94.5 4.9 copy-start.2
  111.3 4.9 copy-start.2
  128.1 4.9 copy-start.2
  144.9 4.9 copy-start.2
  161.7 4.9 copy-start.2
  178.6 4.9 copy-start.2
  214.3 1279.2 %all-to-all-start.1 = ((bf16[64,2,896,64]{2,3,1,0:T(8,128)(2,1)}), bf16[64,2,896,64]{2,3,1,0:T(8,128)(2,1)}, u32[]{:S(2)}, u32[]{:S(2)}) async-start(bf16[64,2,896,64]{2,3,1,0:T(8,128)(2,1)} %broadcast_multiply_fusion), calls=%async_computation.1 | async-start | bytes 29360128 | tf_op jit(solution)/shard_map/all_to_all | solution.py:107
  1568.3 35.5 %copy-start.4 = (f32[448,32,32]{0,2,1:T(8,128)S(1)}, f32[448,32,32]{0,2,1:T(8,128)}, u32[]{:S(2)}) copy-start(f32[448,32,32]{0,2,1:T(8,128)} %copy-done.3) | copy-start | bytes 5505028
  1568.3 35.5 %copy-start.6 = (f32[448,32,32]{0,2,1:T(8,128)S(1)}, f32[448,32,32]{0,2,1:T(8,128)}, u32[]{:S(2)}) copy-start(f32[448,32,32]{0,2,1:T(8,128)} %copy-done.5) | copy-start | bytes 5505028
  1568.3 35.5 %copy-start.8 = (f32[448,32,32]{0,2,1:T(8,128)S(1)}, f32[448,32,32]{0,2,1:T(8,128)}, u32[]{:S(2)}) copy-start(f32[448,32,32]{0,2,1:T(8,128)} %copy-done.7) | copy-start | bytes 5505028
  1615.2 31.3 %copy-start.11 = (f32[448,32]{0,1:T(8,128)S(1)}, f32[448,32]{0,1:T(8,128)}, u32[]{:S(2)}) copy-start(f32[448,32]{0,1:T(8,128)} %copy-done.10) | copy-start | bytes 172036
  1615.2 31.3 %copy-start.13 = (f32[448,32]{0,1:T(8,128)S(1)}, f32[448,32]{0,1:T(8,128)}, u32[]{:S(2)}) copy-start(f32[448,32]{0,1:T(8,128)} %copy-done.12) | copy-start | bytes 172036
  1615.2 31.3 %copy-start.15 = (f32[448,32]{0,1:T(8,128)S(1)}, f32[448,32]{0,1:T(8,128)}, u32[]{:S(2)}) copy-start(f32[448,32]{0,1:T(8,128)} %copy-done.14) | copy-start | bytes 172036
  1615.2 31.3 %copy-start.17 = (f32[448,32]{0,1:T(8,128)S(1)}, f32[448,32]{0,1:T(8,128)}, u32[]{:S(2)}) copy-start(f32[448,32]{0,1:T(8,128)} %copy-done.16) | copy-start | bytes 172036
  1618.6 50.1 %all-to-all-start.2 = ((f32[64,1,32]{2,1,0:T(1,128)}), f32[64,1,32]{2,1,0:T(1,128)S(1)}, u32[]{:S(2)}, u32[]{:S(2)}) async-start(f32[64,1,32]{2,1,0:T(1,128)} %broadcast_in_dim.14), calls=%async_computation.2 | async-start | bytes 65536 | tf_op jit(solution)/shard_map/all_to_all | solution.py:14
  1649.1 20.2 %copy-start.1 = (f32[2,448,256]{2,1,0:T(8,128)S(1)}, f32[2,448,256]{2,1,0:T(8,128)}, u32[]{:S(2)}) copy-start(f32[2,448,256]{2,1,0:T(8,128)} %param.14) | copy-start | bytes 2752516
  (7 other events, 8.2 us)
where the time goes:
time: 1670 us
  waiting for transfers between devices  1270 us (76%)
  local copies, waits for them, and re-layouts  175 us (10%)
  matrix products  94.1 us (6%)
  starting transfers between devices  86.1 us (5%)
  other arithmetic  42.9 us (3%)
    all_to_all x1, waiting for transfers between devices, shards(): lax.all_to_all(outgoing, 'sph', split_axis=0, concat_axis=0, tiled=True)  1250 us
    gather x8, local copies, waits for them, and re-layouts, one_group(): tables = trans_table[picked]  56.2 us
    dot_general x1, matrix products, shards(): jnp.dot(gather_matrix, partial_value.reshape(slot_count, 2 * mode_count *...  35.5 us
    all_to_all x1, starting transfers between devices, shards(): lax.all_to_all(slot_target.reshape(devices, capacity), 'sph', split_axis=...  34.9 us
  transfers between devices with their start and end apart: 3, of which 2 were waited for; matrix products, arithmetic and copies ran while one was open for 11% of the time, Pallas kernels for 0%

commit v1 on v0

v1 whole, which is shorter than its diff:
```python
import functools

import jax
import jax.numpy as jnp
from jax import lax
from jax.experimental import pallas as pl
from jax.experimental.pallas import tpu as pltpu
from jax.sharding import PartitionSpec as P

BLOCK = 2
LANES = 128
F32 = jnp.float32
BF16 = jnp.bfloat16
HIGHEST = lax.Precision.HIGHEST
NT = (((1,), (1,)), ((), ()))


def iota(shape, axis):
    return lax.broadcasted_iota(jnp.int32, shape, axis)


def split3(x):
    hi = x.astype(BF16)
    rest = x - hi.astype(F32)
    mid = rest.astype(BF16)
    low = (rest - mid.astype(F32)).astype(BF16)
    return hi, mid, low


def pack_kernel(mie_ref, pos_ref, route_ref, source_ref, target_ref, class_ref, out_ref):
    dests = out_ref.shape[1]
    pairs = route_ref.shape[1]
    spheres = pos_ref.shape[0]
    named = (route_ref[...] == iota((dests, pairs), 0)).astype(BF16)
    earlier = (iota((pairs, pairs), 0) < iota((pairs, pairs), 1)).astype(BF16)
    before = jnp.dot(named, earlier, preferred_element_type=F32)
    pos = pos_ref[...]
    hi, mid, low = (part.astype(F32) for part in split3(pos))
    lane = iota(pos.shape, 1)
    pos_parts = jnp.where(lane < 3, hi, jnp.where(lane < 6, mid, low)).astype(BF16)
    row = iota((LANES, pairs), 0)
    pair_meta = jnp.where(
        row == 9, target_ref[...] + 1, jnp.where(row == 10, class_ref[...], 0)
    ).astype(F32).astype(BF16)
    for r in range(2):
        slot = jnp.where(before == float(r), named.astype(F32), 0.0).astype(BF16)
        meta = lax.dot_general(slot, pair_meta, NT, preferred_element_type=F32)
        for s in range(2):
            origin = (source_ref[...] * BLOCK + s == iota((spheres, pairs), 0)).astype(F32).astype(BF16)
            pick = lax.dot_general(slot, origin, NT, preferred_element_type=F32).astype(BF16)
            where = jnp.dot(pick, pos_parts, preferred_element_type=F32)
            units = mie_ref.shape[0] // LANES
            for u in range(units):
                rows = mie_ref[u * LANES : (u + 1) * LANES, :].astype(BF16)
                out_ref[2 * r + s, :, u, :] = lax.dot_general(pick, rows, NT, preferred_element_type=F32).astype(BF16)
            out_ref[2 * r + s, :, units, :] = (where + meta).astype(BF16)


def field_kernel(
    slots_ref, pattern_ref, wave_ref, dirs_ref, own_ref, mie_ref, table_ref, out_ref, ext_ref,
    left, weights, x_buf, z_buf, pat, mie_wide,
):
    modes = table_ref.shape[2]
    both = 2 * modes
    sources = slots_ref.shape[1]
    slots = 2 * sources
    columns = out_ref.shape[1]
    half = columns // 2
    classes = table_ref.shape[0]
    dirs = LANES // 4
    select = (iota((pattern_ref.shape[1], LANES), 0) == dirs_ref[...]).astype(F32)
    pat[...] = jnp.dot(pattern_ref[...], select, precision=HIGHEST, preferred_element_type=F32)
    waves = jnp.dot(wave_ref[...], select, precision=HIGHEST, preferred_element_type=F32)
    kx, ky, kz = waves[0:1], waves[1:2], waves[2:3]

    wide = iota((mie_ref.shape[1], columns), 1)
    sphere_of = (wide // dirs) % (half // dirs) * BLOCK + wide // half
    spread = (iota(wide.shape, 0) == sphere_of).astype(F32).astype(BF16)
    total = None
    for part in split3(mie_ref[...]):
        term = jnp.dot(part, spread, preferred_element_type=F32)
        total = term if total is None else total + term
    mie_wide[...] = total

    units = both // LANES
    phases = []
    for s in range(2):
        for u in range(units):
            block = jnp.concatenate(
                [slots_ref[s, :, u, :].astype(F32), slots_ref[2 + s, :, u, :].astype(F32)], 0
            )
            left[s, u * LANES : (u + 1) * LANES, 0:slots] = block.T.astype(BF16)
        left[s, 0:modes, slots : 2 * slots] = -left[s, modes:both, 0:slots]
        left[s, modes:both, slots : 2 * slots] = left[s, 0:modes, 0:slots]
        meta = jnp.concatenate(
            [slots_ref[s, :, units, :].astype(F32), slots_ref[2 + s, :, units, :].astype(F32)], 0
        )
        x = meta[:, 0:1] + meta[:, 3:4] + meta[:, 6:7]
        y = meta[:, 1:2] + meta[:, 4:5] + meta[:, 7:8]
        z = meta[:, 2:3] + meta[:, 5:6] + meta[:, 8:9]
        phase = x * kx + y * ky + z * kz
        phases.append((jnp.cos(phase), jnp.sin(phase)))
        code = meta[:, 10:11] * float(half // dirs) + meta[:, 9:10] - 1.0
        code = jnp.where(meta[:, 9:10] > 0.0, code, -1.0)
    code = jnp.broadcast_to(code, (slots, LANES))

    def one_class(c, carry):
        for s in range(2):
            cosine, sine = phases[s]
            for t in range(half // LANES):
                block_of = (iota((slots, LANES), 1) // dirs + t * (LANES // dirs) + c * (half // dirs)).astype(F32)
                hit = code == block_of
                weights[0:slots, t * LANES : (t + 1) * LANES] = jnp.where(hit, cosine, 0.0).astype(BF16)
                weights[slots : 2 * slots, t * LANES : (t + 1) * LANES] = jnp.where(hit, sine, 0.0).astype(BF16)
            for n in range(half // 256):
                cut = slice(n * 256, (n + 1) * 256)
                gathered = jnp.dot(left[s], weights[:, cut], preferred_element_type=F32)
                for t in range(2):
                    lanes = slice(t * LANES, (t + 1) * LANES)
                    g_real, g_imag = gathered[:modes, lanes], gathered[modes:, lanes]
                    p_real, p_imag = pat[:modes, :], pat[modes:, :]
                    at = s * half + n * 256 + t * LANES
                    x_buf[:, at : at + LANES] = (g_real * p_real - g_imag * p_imag).astype(BF16)
                    x_buf[:, columns + at : columns + at + LANES] = (g_real * p_imag + g_imag * p_real).astype(BF16)
        matrix = table_ref[c].reshape(both, modes)

        def one_cut(n, carry):
            at = pl.ds(pl.multiple_of(n * 512, 512), 512)
            z_buf[:, at] += jnp.dot(matrix, x_buf[:, at], preferred_element_type=F32)
            return carry

        return lax.fori_loop(0, 2 * columns // 512, one_cut, carry)

    z_buf[...] = jnp.zeros_like(z_buf)
    lax.fori_loop(0, classes, one_class, 0)

    order_in, order_out = iota((256, 256), 0), iota((256, 256), 1)
    wanted = (order_out // dirs) % 2 * LANES + order_out // (2 * dirs) * dirs + order_out % dirs
    shuffle = (order_in == wanted).astype(F32).astype(BF16)
    ext = jnp.zeros((8, LANES), F32)
    for t in range(half // LANES):
        parts = []
        for s in range(2):
            at = s * half + t * LANES
            lanes = slice(at, at + LANES)
            own = slice(columns + at, columns + at + LANES)
            phase = own_ref[0:1, lanes] * kx + own_ref[1:2, lanes] * ky + own_ref[2:3, lanes] * kz
            cosine, sine = jnp.cos(phase), jnp.sin(phase)
            p_real, p_imag = pat[:modes, :], pat[modes:, :]
            inc_real = cosine * p_real - sine * p_imag
            inc_imag = cosine * p_imag + sine * p_real
            tot_real = inc_real + (z_buf[:modes, lanes] - z_buf[modes:, own])
            tot_imag = inc_imag + (z_buf[modes:, lanes] + z_buf[:modes, own])
            m_real, m_imag = mie_wide[:modes, lanes], mie_wide[modes:, lanes]
            o_real = m_real * tot_real - m_imag * tot_imag
            o_imag = m_real * tot_imag + m_imag * tot_real
            ext += (inc_real * o_real + inc_imag * o_imag).reshape(modes // 8, 8, LANES).sum(0)
            parts.append((o_real.astype(BF16), o_imag.astype(BF16)))
        out = slice(t * 256, (t + 1) * 256)
        for k in range(2):
            mixed = jnp.concatenate([parts[0][k], parts[1][k]], 1)
            out_ref[k * modes : (k + 1) * modes, out] = jnp.dot(
                mixed, shuffle, preferred_element_type=F32
            ).astype(BF16)
    ext_ref[...] = ext


def shards(
    positions, wave_vectors, pattern, dir_index, mie, trans_table, pair_route, pair_source, pair_target, pair_class,
):
    modes = pattern.shape[1]
    spheres = positions.shape[0]
    dirs = dir_index.shape[0]
    devices = lax.axis_size("sph")
    groups = lax.axis_size("groups")
    pairs = pair_source.shape[0]
    columns = spheres * dirs
    units = 2 * modes // LANES + 1
    mie = mie.reshape(2 * modes, spheres)
    pattern = pattern.reshape(2 * modes, -1)
    pos_wide = jnp.pad(jnp.concatenate([positions] * 3, 1), ((0, 0), (0, LANES - 9)))
    wave_rows = jnp.pad(wave_vectors.T, ((0, 5), (0, 0)))
    dir_row = jnp.tile(dir_index, LANES // dirs)[None]
    own = jnp.broadcast_to(
        positions.reshape(spheres // BLOCK, BLOCK, 3).transpose(2, 1, 0)[..., None], (3, BLOCK, spheres // BLOCK, dirs)
    ).reshape(3, columns)
    own = jnp.pad(own, ((0, 5), (0, 0)))
    vmem = pl.BlockSpec(memory_space=pltpu.VMEM)
    packed = pl.pallas_call(
        pack_kernel,
        out_shape=jax.ShapeDtypeStruct((4, devices, units, LANES), BF16),
        in_specs=[vmem] * 6,
        out_specs=vmem,
        name="pack",
    )(mie, pos_wide, pair_route.reshape(1, pairs), pair_source[None], pair_target[None], pair_class[None])
    share = packed.transpose(1, 0, 2, 3).reshape(devices, groups, 4 * units * LANES // groups)
    share = lax.dynamic_index_in_dim(share, lax.axis_index("groups"), 1, keepdims=False)
    arrived = lax.all_to_all(share, "sph", split_axis=0, concat_axis=0, tiled=True)
    slots = lax.all_gather(arrived, "groups", axis=1, tiled=False)
    slots = slots.reshape(devices, 4, units, LANES).transpose(1, 0, 2, 3)
    scattered, ext = pl.pallas_call(
        field_kernel,
        out_shape=(
            jax.ShapeDtypeStruct((2 * modes, columns), BF16),
            jax.ShapeDtypeStruct((8, LANES), F32),
        ),
        in_specs=[vmem] * 7,
        out_specs=(vmem, vmem),
        scratch_shapes=[
            pltpu.VMEM((2, 2 * modes, 4 * devices), BF16),
            pltpu.VMEM((4 * devices, columns // 2), BF16),
            pltpu.VMEM((modes, 2 * columns), BF16),
            pltpu.VMEM((2 * modes, 2 * columns), F32),
            pltpu.VMEM((2 * modes, LANES), F32),
            pltpu.VMEM((2 * modes, columns), F32),
        ],
        compiler_params=pltpu.CompilerParams(vmem_limit_bytes=60 * 1024 * 1024),
        name="field",
    )(slots, pattern, wave_rows, dir_row, own, mie, trans_table)
    local = ext.sum(0).reshape(LANES // dirs, dirs).sum(0)
    copies = jnp.broadcast_to(local, (devices, dirs))
    extinction = lax.all_to_all(copies, "sph", split_axis=0, concat_axis=0, tiled=True).sum(0)
    return (scattered, extinction)


def solution(mesh):
    placed = (
        P("sph", None),
        P(),
        P(),
        P("groups"),
        P(None, None, "sph"),
        P(),
        P("sph", None),
        P("sph"),
        P("sph"),
        P("sph"),
    )
    return jax.shard_map(
        shards,
        mesh=mesh,
        in_specs=placed,
        out_specs=(P(None, ("groups", "sph")), P("groups")),
        check_vma=False,
    )
```

time: 1670 us -> 158 us (0.09)
  waiting for transfers between devices: 1270 us -> 25.8 us
  local copies, waits for them, and re-layouts: 175 us -> 10.5 us
  matrix products: 94.1 us -> 0 us
  starting transfers between devices: 86.1 us -> 34.3 us
  Pallas kernels: 0 us -> 44 us
  other arithmetic: 42.9 us -> 2.65 us
  blocking collectives: 0 us -> 39.2 us
    all_to_all x3 -> x1, waiting for transfers between devices: 1270 us -> 25.8 us  [shards(): lax.all_to_all(share, 'sph', split_axis=0, concat_axis=0, tiled=True)]
    dot_general x35 -> x0, matrix products: 94.1 us -> none  [the longest x1 35.5 us: shards(): jnp.dot(gather_matrix, partial_value.reshape(slot_count, 2 * mode_count *...]
    gather x11 -> x0, local copies, waits for them, and re-layouts: 74.3 us -> none  [the longest x8 56.2 us: one_group(): tables = trans_table[picked]]
    all_to_all x3 -> x1, starting transfers between devices: 86.1 us -> 34.3 us  [shards(): lax.all_to_all(share, 'sph', split_axis=0, concat_axis=0, tiled=True)]
    pallas_call x0 -> x2, Pallas kernels: none -> 44 us  [the longest x1 40 us: shards(): pl.pallas_call(field_kernel, out_shape=(jax.ShapeDtypeStruct((2 * modes,...]
    all_to_all x0 -> x1, blocking collectives: none -> 29.9 us  [shards(): lax.all_to_all(copies, 'sph', split_axis=0, concat_axis=0, tiled=True)]
    all_to_all x2 -> x1, local copies, waits for them, and re-layouts: 27 us -> 0.05 us  [shards(): lax.all_to_all(share, 'sph', split_axis=0, concat_axis=0, tiled=True)]
    another operation x1 -> x2, local copies, waits for them, and re-layouts: 28.1 us -> 1.25 us  [shards(): dir_row = jnp.tile(dir_index, LANES // dirs)[None]]
  transfers between devices with their start and end apart: 3 -> 1, of which waited for: 2 -> 1; matrix products, arithmetic and copies ran while one was open for 11% -> 3% of each run, Pallas kernels for 0% -> 0%
where the time goes in v1:
time: 158 us; the launch traced here: 157 us
  Pallas kernels  44 us (28%)
  blocking collectives  39.2 us (25%)
  starting transfers between devices  34.3 us (22%)
  waiting for transfers between devices  25.8 us (16%)
  local copies, waits for them, and re-layouts  10.5 us (7%)
  other arithmetic  2.65 us (2%)
    pallas_call x1, Pallas kernels, shards(): pl.pallas_call(field_kernel, out_shape=(jax.ShapeDtypeStruct((2 * modes,...  40 us
    all_to_all x1, starting transfers between devices, shards(): lax.all_to_all(share, 'sph', split_axis=0, concat_axis=0, tiled=True)  34.3 us
    all_to_all x1, blocking collectives, shards(): lax.all_to_all(copies, 'sph', split_axis=0, concat_axis=0, tiled=True)  29.9 us
    all_to_all x1, waiting for transfers between devices, shards(): lax.all_to_all(share, 'sph', split_axis=0, concat_axis=0, tiled=True)  25.8 us
    all_gather x1, blocking collectives, shards(): slots = lax.all_gather(arrived, 'groups', axis=1, tiled=False)  9.3 us
    unnamed x6, local copies, waits for them, and re-layouts  4.87 us
    pallas_call x1, Pallas kernels, shards(): pl.pallas_call(pack_kernel, out_shape=jax.ShapeDtypeStruct((4, devices, u...  3.94 us
  transfers between devices with their start and end apart: 1, of which 1 were waited for; matrix products, arithmetic and copies ran while one was open for 3% of the time, Pallas kernels for 0%

profile of v1, /device:TPU:37, one launch (start us, length us, event | category | flops | bytes accessed | tf_op | source)
XLA Modules:
  0.0 157.1 jit_solution(15061994753002435963)
XLA Ops:
  0.6 0.8 copy.37
  1.4 0.7 select_maximum_fusion.pos_ref
  2.1 1.9 %copy.36 = f32[2,448,32]{2,1,0:T(8,128)} copy(f32[2,448,32]{1,2,0:T(8,128)} %param.14) | data formatting | bytes 229376 | tf_op args[4]
  3.9 3.9 %pack.1 = bf16[4,64,8,128]{3,2,1,0:T(8,128)(2,1)} custom-call(f32[896,32]{1,0:T(8,128)} %bitcast.25, f32[32,128]{1,0:T(8,128)} %select_maximum_fusion.pos_ref, s32[1,64]{1,0:T(1,128)} %bitcast.33, s32[1,64]{1,0:T(1,128)} %bitcast.34, s32[1,64]{1,0:T(1,128)} %bitcast.35, s32[1,64]{1,0:T(1,128)} %bitcast.36), custom_call_target="tpu_custom_call" | custom-call | tf_op jit(solution)/shard_map/pack/pallas_call | solution.py:189
  7.9 1.3 reshape.40
  9.2 0.5 broadcast.19
  9.7 0.7 reduce.1
  10.4 0.7 reshape.46
  11.1 34.3 %all-to-all-start = ((bf16[64,2,512]{2,1,0:T(2,128)(2,1)}), bf16[64,2,512]{2,1,0:T(2,128)(2,1)S(1)}, u32[]{:S(2)}, u32[]{:S(2)}) async-start(bf16[64,2,512]{2,1,0:T(2,128)(2,1)} %reshape.46), calls=%async_computation | async-start | bytes 262144 | tf_op jit(solution)/shard_map/all_to_all | solution.py:198
  45.4 0.8 reshape.43
  46.2 0.7 tile.2
  46.9 0.6 broadcast_in_dim_tile.3.dirs_ref
  47.5 0.1 copy.42
  47.6 0.1 reshape.44
  47.7 1.3 pad.13.wave_ref
  49.0 0.6 pad.14.own_ref
  49.7 25.8 %all-to-all-done = bf16[64,2,512]{2,1,0:T(2,128)(2,1)S(1)} async-done(((bf16[64,2,512]{2,1,0:T(2,128)(2,1)}), bf16[64,2,512]{2,1,0:T(2,128)(2,1)S(1)}, u32[]{:S(2)}, u32[]{:S(2)}) %all-to-all-start) | async-done | bytes 131104 | tf_op jit(solution)/shard_map/all_to_all | solution.py:198
  75.5 0.1 reshape.47
  75.6 9.3 %all_gather.4 = bf16[64,4,1024]{2,0,1:T(8,128)(2,1)S(1)} all-gather(bf16[64,1,1024]{2,0,1:T(8,128)(2,1)S(1)} %copy.41), channel_id=1, replica_groups=mesh['groups'=4,'sph'=64] {'groups'}, dimensions={1}, use_global_device_ids=true | all-gather | bytes 655360 | tf_op jit(solution)/shard_map/all_gather | solution.py:199
  84.9 0.9 copy.46
  85.8 40.0 %field.1 = (bf16[896,1024]{1,0:T(8,128)(2,1)}, f32[8,128]{1,0:T(8,128)}) custom-call(bf16[4,64,8,128]{3,2,1,0:T(8,128)(2,1)} %bitcast.29, f32[896,256]{1,0:T(8,128)} %bitcast.30, f32[8,256]{1,0:T(8,128)} %pad.13.wave_ref, s32[1,128]{1,0:T(1,128)} %broadcast_in_dim_tile.3.dirs_ref, f32[8,1024]{1,0:T(8,128)} %pad.14.own_ref, f32[896,32]{1,0:T(8,128)} %bitcast.26, ...), custom_call_target="tpu_custom_call" | custom-call | tf_op jit(solution)/shard_map/field/pallas_call | solution.py:201
  125.8 0.7 reduce_sum.27
  126.6 29.9 %all_to_all.12 = f32[64,1,32]{2,1,0:T(1,128)S(1)} all-to-all(f32[64,1,32]{2,1,0:T(1,128)S(1)} %broadcast_in_dim.22), channel_id=1, replica_groups=mesh['groups'=4,'sph'=64] {'sph'}, dimensions={0} | all-to-all | bytes 16384 | tf_op jit(solution)/shard_map/all_to_all | solution.py:222
  156.5 0.6 reduce_sum.29
  (6 shorter events, 0.3 us)
Async XLA Ops:
  11.1 64.4 %all-to-all-start = ((bf16[64,2,512]{2,1,0:T(2,128)(2,1)}), bf16[64,2,512]{2,1,0:T(2,128)(2,1)S(1)}, u32[]{:S(2)}, u32[]{:S(2)}) async-start(bf16[64,2,512]{2,1,0:T(2,128)(2,1)} %reshape.46), calls=%async_computation | async-start | bytes 262144 | tf_op jit(solution)/shard_map/all_to_all | solution.py:198

commit v2 on v1

v2 whole, which is shorter than its diff:
```python
import jax
import jax.numpy as jnp
from jax import lax
from jax.experimental import pallas as pl
from jax.experimental.pallas import tpu as pltpu
from jax.sharding import PartitionSpec as P

BLOCK = 2
LANES = 128
WIDE = 256
PART = 8
TARGET_AT = 24
CLASS_AT = 25
F32 = jnp.float32
BF16 = jnp.bfloat16
HIGHEST = lax.Precision.HIGHEST
MESH = pl.DeviceIdType.MESH
NT = (((1,), (1,)), ((), ()))


def iota(shape, axis):
    return lax.broadcasted_iota(jnp.int32, shape, axis)


def ones_where(mask):
    return mask.astype(F32).astype(BF16)


def split3(x):
    hi = x.astype(BF16)
    rest = x - hi.astype(F32)
    mid = rest.astype(BF16)
    low = (rest - mid.astype(F32)).astype(BF16)
    return hi, mid, low


def dot(a, b, **kw):
    return jnp.dot(a, b, preferred_element_type=F32, **kw)


def body(
    route_ref, source_ref, target_ref, class_ref, pos_ref, wave_ref, dirs_ref, mie_ref, pattern_ref, table_hbm,
    out_ref, ext_ref,
    send, recv, ext_send, ext_recv, table, table_sem, send_sem, recv_sem, gsend_sem, grecv_sem, esend_sem, erecv_sem,
    parts, mie_rows, pat, mie_wide, inc, base, left, weights, matrix, x_all,
):
    me = lax.axis_index("sph")
    group = lax.axis_index("groups")
    devices = lax.axis_size("sph")
    groups = lax.axis_size("groups")
    pairs = route_ref.shape[1]
    spheres, modes = mie_ref.shape[1:]
    both = 2 * modes
    classes = table.shape[0]
    columns = out_ref.shape[1]
    dirs = dirs_ref.shape[1]
    blocks = spheres // BLOCK
    tile_blocks = LANES // dirs
    tiles = blocks // tile_blocks
    slots = 2 * devices
    units = both // LANES + 1
    share = recv.shape[2]
    whole = modes // LANES

    barrier = pltpu.get_barrier_semaphore()

    def greet(i, carry):
        pl.semaphore_signal(barrier, inc=1, device_id={"sph": lax.rem(me + i, devices)}, device_id_type=MESH)
        return carry

    def greet_group(i, carry):
        pl.semaphore_signal(barrier, inc=1, device_id={"groups": lax.rem(group + i, groups)}, device_id_type=MESH)
        return carry

    lax.fori_loop(1, devices, greet, 0)
    lax.fori_loop(1, groups, greet_group, 0)
    load_table = pltpu.make_async_copy(table_hbm, table, table_sem)
    load_table.start()

    named = ones_where(route_ref[...] == iota((devices, pairs), 0))
    earlier = ones_where(iota((pairs, pairs), 0) < iota((pairs, pairs), 1))
    before = dot(named, earlier)
    parts[...] = jnp.zeros_like(parts)
    for i, part in enumerate(split3(pos_ref[...])):
        parts[i * PART : i * PART + 3, :] = part.astype(F32)
    row = iota((LANES, pairs), 0)
    pair_meta = jnp.where(
        row == TARGET_AT, target_ref[...] + 1, jnp.where(row == CLASS_AT, class_ref[...], 0)
    ).astype(F32).astype(BF16)
    mixed = jnp.concatenate([mie_ref[0, :, whole * LANES :], mie_ref[1, :, whole * LANES :]], 1)
    first_unit = group * share
    rows_of_share = max(1, share // units)
    for n in range(rows_of_share):
        kind = first_unit // units + n
        rank = (kind // 2).astype(F32)
        sphere = lax.rem(kind, 2)
        slot = jnp.where(before == rank, named.astype(F32), 0.0).astype(BF16)
        origin = ones_where(source_ref[...] * BLOCK + sphere == iota((spheres, pairs), 0))
        pick = lax.dot_general(slot, origin, NT, preferred_element_type=F32).astype(BF16)
        meta = lax.dot_general(slot, pair_meta, NT, preferred_element_type=F32)
        where = lax.dot_general(pick, parts[...].astype(BF16), NT, preferred_element_type=F32)
        for u in range(units):
            if u == units - 1:
                value = where + meta
            else:
                c, t = divmod(u, whole)
                rows = mixed if c == 2 else mie_ref[c, :, t * LANES : (t + 1) * LANES]
                value = dot(pick, rows.astype(BF16))
            at = n * units + u
            send[at // share, :, at % share, :] = value.astype(BF16)
    piece = lax.rem(first_unit, units) // share if share < units else 0

    pl.semaphore_wait(barrier, devices + groups - 2)

    def offset_of(i):
        return devices // 2 + (i + 1) // 2 * (1 - 2 * lax.rem(i, 2))

    def exchange(src, dst, sends, receives, offset):
        return pltpu.make_async_remote_copy(
            src_ref=src,
            dst_ref=dst,
            send_sem=sends.at[offset],
            recv_sem=receives.at[offset],
            device_id={"sph": lax.rem(me + offset, devices)},
            device_id_type=MESH,
        )

    def slot_copy(i, landing):
        offset = offset_of(i)
        to = lax.rem(me + offset, devices)
        here = lax.rem(me + devices - offset, devices) if landing else me
        return exchange(send.at[piece, to], recv.at[group, here], send_sem, recv_sem, offset)

    def start_slot(i, carry):
        slot_copy(i, False).start()
        return carry

    lax.fori_loop(0, devices - 1, start_slot, 0)
    recv[group, me] = send[piece, me]

    lane_dir = dirs_ref[...]
    lane_dirs = jnp.concatenate([lane_dir] * tile_blocks, 1)
    select = (iota((pattern_ref.shape[1], LANES), 0) == lane_dirs).astype(F32)
    pat[...] = dot(pattern_ref[...], select, precision=HIGHEST)
    waves = dot(wave_ref[...], select, precision=HIGHEST)
    kx, ky, kz = waves[0:1], waves[1:2], waves[2:3]
    wide = iota((LANES, columns), 1)
    sphere_of = ((wide // WIDE) * tile_blocks + wide // dirs % tile_blocks) * BLOCK + wide // LANES % BLOCK
    spread = ones_where(lax.rem(iota((LANES, columns), 0), spheres) == sphere_of)
    own = dot(pos_ref[...], spread[0:spheres].astype(F32), precision=HIGHEST)
    mie_rows[...] = jnp.zeros_like(mie_rows)
    for c in range(2):
        for i, part in enumerate(split3(mie_ref[c])):
            mie_rows[i * spheres : (i + 1) * spheres, 0:modes] = part.astype(F32)
        mie_wide[c * modes : (c + 1) * modes, :] = dot(mie_rows[...].T[:modes].astype(BF16), spread)
    for n in range(columns // LANES):
        lanes = slice(n * LANES, (n + 1) * LANES)
        phase = own[0:1, lanes] * kx + own[1:2, lanes] * ky + own[2:3, lanes] * kz
        cosine, sine = jnp.cos(phase), jnp.sin(phase)
        p_real, p_imag = pat[:modes, :], pat[modes:, :]
        i_real = cosine * p_real - sine * p_imag
        i_imag = cosine * p_imag + sine * p_real
        m_real, m_imag = mie_wide[:modes, lanes], mie_wide[modes:, lanes]
        inc[:modes, lanes] = i_real
        inc[modes:, lanes] = i_imag
        base[:modes, lanes] = m_real * i_real - m_imag * i_imag
        base[modes:, lanes] = m_real * i_imag + m_imag * i_real
    load_table.wait()
    for c in range(classes // 2):
        matrix[:, c * both : (c + 1) * both] = jnp.concatenate([table[2 * c], table[2 * c + 1]], 1)

    def end_slot(i, carry):
        copy = slot_copy(i, True)
        copy.wait_send()
        copy.wait_recv()
        return carry

    lax.fori_loop(0, devices - 1, end_slot, 0)

    def share_copy(i, landing):
        at = lax.rem(group + groups - i, groups) if landing else group
        return pltpu.make_async_remote_copy(
            src_ref=recv.at[group],
            dst_ref=recv.at[at],
            send_sem=gsend_sem.at[i],
            recv_sem=grecv_sem.at[i],
            device_id={"groups": lax.rem(group + i, groups)},
            device_id_type=MESH,
        )

    def start_share(i, carry):
        share_copy(i, False).start()
        return carry

    def end_share(i, carry):
        copy = share_copy(i, True)
        copy.wait_send()
        copy.wait_recv()
        return carry

    lax.fori_loop(1, groups, start_share, 0)
    lax.fori_loop(1, groups, end_share, 0)

    def arrived(s, u):
        both_ranks = []
        for r in range(2):
            at = (2 * r + s) * units + u
            both_ranks.append(recv[at // share, :, at % share, :].astype(F32))
        return jnp.concatenate(both_ranks, 0)

    phases = []
    for s in range(2):
        for u in range(units - 1):
            c, t = divmod(u, whole)
            block = arrived(s, u).T.astype(BF16)
            if c < 2:
                at = c * modes + t * LANES
                left[s, at : at + LANES, 0:slots] = block
            else:
                rest = modes - whole * LANES
                left[s, whole * LANES : modes, 0:slots] = block[:rest]
                left[s, modes + whole * LANES : both, 0:slots] = block[rest:]
        left[s, 0:modes, slots : 2 * slots] = -left[s, modes:both, 0:slots]
        left[s, modes:both, slots : 2 * slots] = left[s, 0:modes, 0:slots]
        meta = arrived(s, units - 1)
        x, y, z = (
            meta[:, i : i + 1] + meta[:, PART + i : PART + i + 1] + meta[:, 2 * PART + i : 2 * PART + i + 1]
            for i in range(3)
        )
        phase = x * kx + y * ky + z * kz
        phases.append((jnp.cos(phase), jnp.sin(phase)))
    target = meta[:, TARGET_AT : TARGET_AT + 1]
    code = jnp.where(target > 0.0, meta[:, CLASS_AT : CLASS_AT + 1] * float(blocks) + target - 1.0, -1.0)
    code = jnp.broadcast_to(code, (slots, LANES))

    def form(c, carry):
        rows = pl.ds(pl.multiple_of(c * modes, 64), modes)
        for s in range(2):
            cosine, sine = phases[s]
            for t in range(tiles):
                block_of = (iota((slots, LANES), 1) // dirs + t * tile_blocks + c * blocks).astype(F32)
                hit = code == block_of
                lanes = slice(t * LANES, (t + 1) * LANES)
                weights[s, 0:slots, lanes] = jnp.where(hit, cosine, 0.0).astype(BF16)
                weights[s, slots : 2 * slots, lanes] = jnp.where(hit, sine, 0.0).astype(BF16)
        for s in range(2):
            for n in range(tiles // 2):
                gathered = dot(left[s], weights[s, :, n * WIDE : (n + 1) * WIDE])
                for t in range(2):
                    lanes = slice(t * LANES, (t + 1) * LANES)
                    g_real, g_imag = gathered[:modes, lanes], gathered[modes:, lanes]
                    p_real, p_imag = pat[:modes, :], pat[modes:, :]
                    at = (2 * n + t) * WIDE + s * LANES
                    x_all[0, rows, at : at + LANES] = (g_real * p_real - g_imag * p_imag).astype(BF16)
                    x_all[1, rows, at : at + LANES] = (g_real * p_imag + g_imag * p_real).astype(BF16)
        return carry

    lax.fori_loop(0, classes, form, 0)

    order_in, order_out = iota((WIDE, WIDE), 0), iota((WIDE, WIDE), 1)
    wanted = order_out // dirs % BLOCK * LANES + order_out // (BLOCK * dirs) * dirs + order_out % dirs
    shuffle = ones_where(order_in == wanted)

    def finish(t, ext):
        lanes = pl.ds(pl.multiple_of(t * WIDE, WIDE), WIDE)
        z_real = dot(matrix[...], x_all[0, :, lanes])
        z_imag = dot(matrix[...], x_all[1, :, lanes])
        y_real = z_real[:modes] - z_imag[modes:]
        y_imag = z_real[modes:] + z_imag[:modes]
        m_real, m_imag = mie_wide[:modes, lanes], mie_wide[modes:, lanes]
        o_real = base[:modes, lanes] + (m_real * y_real - m_imag * y_imag)
        o_imag = base[modes:, lanes] + (m_real * y_imag + m_imag * y_real)
        term = inc[:modes, lanes] * o_real + inc[modes:, lanes] * o_imag
        out_ref[:modes, lanes] = dot(o_real.astype(BF16), shuffle).astype(BF16)
        out_ref[modes:, lanes] = dot(o_imag.astype(BF16), shuffle).astype(BF16)
        return ext + term.reshape(modes // 8, 8, WIDE).sum(0)

    ext = lax.fori_loop(0, tiles, finish, jnp.zeros((8, WIDE), F32))
    local = (ext[:, :LANES] + ext[:, LANES:]).sum(0, keepdims=True)
    ext_send[...] = local
    ext_recv[me] = local

    def ext_copy(i, landing):
        offset = offset_of(i)
        here = lax.rem(me + devices - offset, devices) if landing else me
        return exchange(ext_send, ext_recv.at[here], esend_sem, erecv_sem, offset)

    def start_ext(i, carry):
        ext_copy(i, False).start()
        return carry

    def end_ext(i, carry):
        copy = ext_copy(i, True)
        copy.wait_send()
        copy.wait_recv()
        return carry

    lax.fori_loop(0, devices - 1, start_ext, 0)
    lax.fori_loop(0, devices - 1, end_ext, 0)
    total = jnp.broadcast_to(ext_recv[...].sum(0), (8, LANES))
    shift = LANES // 2
    while shift >= dirs:
        total = total + pltpu.roll(total, shift, 1)
        shift //= 2
    ext_ref[...] = total[0:1, 0:dirs]


def shards(
    positions, wave_vectors, pattern, dir_index, mie, trans_table, pair_route, pair_source, pair_target, pair_class,
):
    modes = pattern.shape[1]
    spheres = positions.shape[0]
    dirs = dir_index.shape[0]
    devices = lax.axis_size("sph")
    groups = lax.axis_size("groups")
    pairs = pair_source.shape[0]
    classes = trans_table.shape[0]
    both = 2 * modes
    columns = spheres * dirs
    units = both // LANES + 1
    share = 4 * units // groups
    slots = 2 * devices
    vmem = pl.BlockSpec(memory_space=pltpu.VMEM)
    dma = pltpu.SemaphoreType.DMA
    scattered, extinction = pl.pallas_call(
        body,
        out_shape=(
            jax.ShapeDtypeStruct((both, columns), BF16),
            jax.ShapeDtypeStruct((1, dirs), F32),
        ),
        in_specs=[vmem] * 9 + [pl.BlockSpec(memory_space=pl.ANY)],
        out_specs=(vmem, vmem),
        scratch_shapes=[
            pltpu.VMEM((max(1, units // share), devices, share, LANES), BF16),
            pltpu.VMEM((groups, devices, share, LANES), BF16),
            pltpu.VMEM((1, LANES), F32),
            pltpu.VMEM((devices, 1, LANES), F32),
            pltpu.VMEM((classes, both, modes), BF16),
            dma,
            dma((devices,)),
            dma((devices,)),
            dma((groups,)),
            dma((groups,)),
            dma((devices,)),
            dma((devices,)),
            pltpu.VMEM((LANES, spheres), F32),
            pltpu.VMEM((LANES, -(-modes // LANES) * LANES), F32),
            pltpu.VMEM((both, LANES), F32),
            pltpu.VMEM((both, columns), F32),
            pltpu.VMEM((both, columns), F32),
            pltpu.VMEM((both, columns), F32),
            pltpu.VMEM((2, both, 2 * slots), BF16),
            pltpu.VMEM((2, 2 * slots, columns // 2), BF16),
            pltpu.VMEM((both, classes * modes), BF16),
            pltpu.VMEM((2, classes * modes, columns), BF16),
        ],
        compiler_params=pltpu.CompilerParams(
            vmem_limit_bytes=63 * 1024 * 1024, collective_id=0, has_side_effects=True
        ),
        name="cluster",
    )(
        pair_route.reshape(1, pairs),
        pair_source[None],
        pair_target[None],
        pair_class[None],
        positions.T,
        wave_vectors.T,
        dir_index[None],
        mie.transpose(0, 2, 1),
        pattern.reshape(both, -1),
        trans_table.reshape(classes, both, modes),
    )
    return (scattered, extinction[0])


def solution(mesh):
    placed = (
        P("sph", None),
        P(),
        P(),
        P("groups"),
        P(None, None, "sph"),
        P(),
        P("sph", None),
        P("sph"),
        P("sph"),
        P("sph"),
    )
    return jax.shard_map(
        shards,
        mesh=mesh,
        in_specs=placed,
        out_specs=(P(None, ("groups", "sph")), P("groups")),
        check_vma=False,
    )
```

time: 158 us -> 105 us (0.66)
  Pallas kernels: 44 us -> 101 us
  blocking collectives: 39.2 us -> 0 us
  starting transfers between devices: 34.3 us -> 0 us
  waiting for transfers between devices: 25.8 us -> 0 us
  local copies, waits for them, and re-layouts: 10.5 us -> 3.39 us
  other arithmetic: 2.65 us -> 0 us
    pallas_call x2 -> x1, Pallas kernels: 44 us -> 101 us  [shards(): pl.pallas_call(body, out_shape=(jax.ShapeDtypeStruct((both, columns), BF1...]
    all_to_all x1 -> x0, starting transfers between devices: 34.3 us -> none  [shards(): lax.all_to_all(share, 'sph', split_axis=0, concat_axis=0, tiled=True)]
    all_to_all x1 -> x0, blocking collectives: 29.9 us -> none  [shards(): lax.all_to_all(copies, 'sph', split_axis=0, concat_axis=0, tiled=True)]
    all_to_all x1 -> x0, waiting for transfers between devices: 25.8 us -> none  [shards(): lax.all_to_all(share, 'sph', split_axis=0, concat_axis=0, tiled=True)]
    all_gather x1 -> x0, blocking collectives: 9.3 us -> none  [shards(): slots = lax.all_gather(arrived, 'groups', axis=1, tiled=False)]
    reshape x4 -> x0, local copies, waits for them, and re-layouts: 2.21 us -> none  [the longest x1 1.26 us: shards(): packed.transpose(1, 0, 2, 3)]
    pad x2 -> x0, local copies, waits for them, and re-layouts: 1.92 us -> none  [the longest x1 1.3 us: shards(): wave_rows = jnp.pad(wave_vectors.T, ((0, 5), (0, 0)))]
    unnamed x6 -> x4, local copies, waits for them, and re-layouts: 4.87 us -> 3.39 us
  transfers between devices with their start and end apart: 1 -> 0, of which waited for: 1 -> 0; matrix products, arithmetic and copies ran while one was open for 3% -> 0% of each run, Pallas kernels for 0% -> 0%
where the time goes in v2:
time: 105 us
  Pallas kernels  101 us (96%)
  local copies, waits for them, and re-layouts  3.39 us (3%)
    pallas_call x1, Pallas kernels, shards(): pl.pallas_call(body, out_shape=(jax.ShapeDtypeStruct((both, columns), BF1...  101 us
    unnamed x4, local copies, waits for them, and re-layouts  3.39 us

profile of v2, /device:TPU:37, one launch (start us, length us, event | category | flops | bytes accessed | tf_op | source)
XLA Modules:
  0.0 105.1 jit_solution(10248372544966235093)
XLA Ops:
  0.6 101.1 %cluster.1 = (bf16[896,1024]{1,0:T(8,128)(2,1)}, f32[1,32]{1,0:T(1,128)}) custom-call(s32[1,64]{1,0:T(1,128)} %bitcast.16, s32[1,64]{1,0:T(1,128)} %bitcast.17, s32[1,64]{1,0:T(1,128)} %bitcast.18, s32[1,64]{1,0:T(1,128)} %bitcast.19, f32[3,32]{1,0:T(4,128)} %bitcast.15, f32[3,256]{1,0:T(4,128)} %bitcast.14, s32[1,32]{1,0:T(1,128)} %bitcast.20, ...), custom_call_target="tpu_custom_call" | custom-call | tf_op jit(solution)/shard_map/cluster/pallas_call | solution.py:325
  101.7 0.0 copy-start
  101.7 2.9 %copy.14 = bf16[896,1024]{1,0:T(8,128)(2,1)} copy(bf16[896,1024]{1,0:T(8,128)(2,1)} %get-tuple-element.8) | data formatting | bytes 3670016
  104.6 0.0 copy-done
  104.6 0.5 copy.15
Async XLA Ops:
  101.7 2.9 %copy-start = (f32[1,32]{1,0:T(1,128)S(1)}, f32[1,32]{1,0:T(1,128)}, u32[]{:S(2)}) copy-start(f32[1,32]{1,0:T(1,128)} %get-tuple-element.5) | copy-start | bytes 388

commit v3 on v2

--- a/solution.py
+++ b/solution.py
@@ -38,9 +38,24 @@
     return jnp.dot(a, b, preferred_element_type=F32, **kw)
 
 
+ROWS = 16
+
+
+def paired(x):
+    return x.reshape(x.shape[0] // (2 * ROWS), 2, ROWS, x.shape[1])
+
+
+def halves(x):
+    groups = paired(x)
+    flat = (x.shape[0] // 2, x.shape[1])
+    return groups[:, 0].reshape(flat), groups[:, 1].reshape(flat)
+
+
 def body(
-    route_ref, source_ref, target_ref, class_ref, pos_ref, wave_ref, dirs_ref, mie_ref, pattern_ref, table_hbm,
-    out_ref, ext_ref,
+    route_hbm, source_hbm, target_hbm, class_hbm, pos_hbm, wave_hbm, dirs_hbm, mie_hbm, pattern_hbm, table_hbm,
+    out_hbm, ext_ref,
+    route_ref, source_ref, target_ref, class_ref, pos_ref, wave_ref, dirs_ref, mie_ref, pattern_ref, load_sem,
+    out_ref, out_sem, z_buf,
     send, recv, ext_send, ext_recv, table, table_sem, send_sem, recv_sem, gsend_sem, grecv_sem, esend_sem, erecv_sem,
     parts, mie_rows, pat, mie_wide, inc, base, left, weights, matrix, x_all,
 ):
@@ -64,18 +79,29 @@
 
     barrier = pltpu.get_barrier_semaphore()
 
+    def offset_of(i):
+        return devices // 2 + (i + 1) // 2 * (1 - 2 * lax.rem(i, 2))
+
     def greet(i, carry):
-        pl.semaphore_signal(barrier, inc=1, device_id={"sph": lax.rem(me + i, devices)}, device_id_type=MESH)
+        to = lax.rem(me + offset_of(i), devices)
+        pl.semaphore_signal(barrier, inc=1, device_id={"sph": to}, device_id_type=MESH)
         return carry
 
     def greet_group(i, carry):
         pl.semaphore_signal(barrier, inc=1, device_id={"groups": lax.rem(group + i, groups)}, device_id_type=MESH)
         return carry
 
-    lax.fori_loop(1, devices, greet, 0)
+    lax.fori_loop(0, devices - 1, greet, 0)
     lax.fori_loop(1, groups, greet_group, 0)
+    given = (route_hbm, source_hbm, target_hbm, class_hbm, pos_hbm, mie_hbm, wave_hbm, dirs_hbm, pattern_hbm)
+    taken = (route_ref, source_ref, target_ref, class_ref, pos_ref, mie_ref, wave_ref, dirs_ref, pattern_ref)
+    loads = [pltpu.make_async_copy(a, b, load_sem.at[i]) for i, (a, b) in enumerate(zip(given, taken))]
     load_table = pltpu.make_async_copy(table_hbm, table, table_sem)
+    for load in loads:
+        load.start()
     load_table.start()
+    for load in loads[:6]:
+        load.wait()
 
     named = ones_where(route_ref[...] == iota((devices, pairs), 0))
     earlier = ones_where(iota((pairs, pairs), 0) < iota((pairs, pairs), 1))
@@ -112,9 +138,6 @@
 
     pl.semaphore_wait(barrier, devices + groups - 2)
 
-    def offset_of(i):
-        return devices // 2 + (i + 1) // 2 * (1 - 2 * lax.rem(i, 2))
-
     def exchange(src, dst, sends, receives, offset):
         return pltpu.make_async_remote_copy(
             src_ref=src,
@@ -125,18 +148,19 @@
             device_id_type=MESH,
         )
 
-    def slot_copy(i, landing):
+    def slot_copy(i):
         offset = offset_of(i)
         to = lax.rem(me + offset, devices)
-        here = lax.rem(me + devices - offset, devices) if landing else me
-        return exchange(send.at[piece, to], recv.at[group, here], send_sem, recv_sem, offset)
+        return exchange(send.at[piece, to], recv.at[group, i], send_sem, recv_sem, offset)
 
     def start_slot(i, carry):
-        slot_copy(i, False).start()
+        slot_copy(i).start()
         return carry
 
     lax.fori_loop(0, devices - 1, start_slot, 0)
-    recv[group, me] = send[piece, me]
+    recv[group, devices - 1] = send[piece, me]
+    for load in loads[6:]:
+        load.wait()
 
     lane_dir = dirs_ref[...]
     lane_dirs = jnp.concatenate([lane_dir] * tile_blocks, 1)
@@ -167,39 +191,51 @@
         base[modes:, lanes] = m_real * i_imag + m_imag * i_real
     load_table.wait()
     for c in range(classes // 2):
-        matrix[:, c * both : (c + 1) * both] = jnp.concatenate([table[2 * c], table[2 * c + 1]], 1)
+        two = jnp.concatenate([table[2 * c], table[2 * c + 1]], 1)
+        for k in range(2):
+            part = two[k * modes : (k + 1) * modes].reshape(modes // ROWS, ROWS, both)
+            matrix[:, k, :, c * both : (c + 1) * both] = part
 
     def end_slot(i, carry):
-        copy = slot_copy(i, True)
+        copy = slot_copy(i)
         copy.wait_send()
         copy.wait_recv()
         return carry
 
-    lax.fori_loop(0, devices - 1, end_slot, 0)
-
-    def share_copy(i, landing):
+    quarter = devices // 4
+
+    def share_copy(q, i, landing):
         at = lax.rem(group + groups - i, groups) if landing else group
+        rows = pl.ds(q * quarter, quarter)
         return pltpu.make_async_remote_copy(
-            src_ref=recv.at[group],
-            dst_ref=recv.at[at],
-            send_sem=gsend_sem.at[i],
-            recv_sem=grecv_sem.at[i],
+            src_ref=recv.at[group, rows],
+            dst_ref=recv.at[at, rows],
+            send_sem=gsend_sem.at[q, i],
+            recv_sem=grecv_sem.at[q, i],
             device_id={"groups": lax.rem(group + i, groups)},
             device_id_type=MESH,
         )
 
-    def start_share(i, carry):
-        share_copy(i, False).start()
-        return carry
-
-    def end_share(i, carry):
-        copy = share_copy(i, True)
-        copy.wait_send()
-        copy.wait_recv()
-        return carry
-
-    lax.fori_loop(1, groups, start_share, 0)
-    lax.fori_loop(1, groups, end_share, 0)
+    def start_share(q, carry):
+        lax.fori_loop(q * quarter, jnp.minimum((q + 1) * quarter, devices - 1), end_slot, 0)
+
+        def start_one(i, carry):
+            share_copy(q, i, False).start()
+            return carry
+
+        return lax.fori_loop(1, groups, start_one, carry)
+
+    def end_share(q, carry):
+        def end_one(i, carry):
+            copy = share_copy(q, i, True)
+            copy.wait_send()
+            copy.wait_recv()
+            return carry
+
+        return lax.fori_loop(1, groups, end_one, carry)
+
+    lax.fori_loop(0, 4, start_share, 0)
+    lax.fori_loop(0, 4, end_share, 0)
 
     def arrived(s, u):
         both_ranks = []
@@ -214,14 +250,17 @@
             c, t = divmod(u, whole)
             block = arrived(s, u).T.astype(BF16)
             if c < 2:
-                at = c * modes + t * LANES
-                left[s, at : at + LANES, 0:slots] = block
+                groups_of = block.reshape(LANES // ROWS, ROWS, slots)
+                at = slice(t * LANES // ROWS, (t + 1) * LANES // ROWS)
+                left[s, at, c, :, 0:slots] = groups_of
+                left[s, at, 1 - c, :, slots : 2 * slots] = -groups_of if c else groups_of
             else:
                 rest = modes - whole * LANES
-                left[s, whole * LANES : modes, 0:slots] = block[:rest]
-                left[s, modes + whole * LANES : both, 0:slots] = block[rest:]
-        left[s, 0:modes, slots : 2 * slots] = -left[s, modes:both, 0:slots]
-        left[s, modes:both, slots : 2 * slots] = left[s, 0:modes, 0:slots]
+                at = slice(whole * LANES // ROWS, modes // ROWS)
+                for c in range(2):
+                    groups_of = block[c * rest : (c + 1) * rest].reshape(rest // ROWS, ROWS, slots)
+                    left[s, at, c, :, 0:slots] = groups_of
+                    left[s, at, 1 - c, :, slots : 2 * slots] = -groups_of if c else groups_of
         meta = arrived(s, units - 1)
         x, y, z = (
             meta[:, i : i + 1] + meta[:, PART + i : PART + i + 1] + meta[:, 2 * PART + i : 2 * PART + i + 1]
@@ -245,10 +284,10 @@
                 weights[s, slots : 2 * slots, lanes] = jnp.where(hit, sine, 0.0).astype(BF16)
         for s in range(2):
             for n in range(tiles // 2):
-                gathered = dot(left[s], weights[s, :, n * WIDE : (n + 1) * WIDE])
+                gathered = dot(left[s].reshape(both, 2 * slots), weights[s, :, n * WIDE : (n + 1) * WIDE])
                 for t in range(2):
                     lanes = slice(t * LANES, (t + 1) * LANES)
-                    g_real, g_imag = gathered[:modes, lanes], gathered[modes:, lanes]
+                    g_real, g_imag = halves(gathered[:, lanes])
                     p_real, p_imag = pat[:modes, :], pat[modes:, :]
                     at = (2 * n + t) * WIDE + s * LANES
                     x_all[0, rows, at : at + LANES] = (g_real * p_real - g_imag * p_imag).astype(BF16)
@@ -257,25 +296,31 @@
 
     lax.fori_loop(0, classes, form, 0)
 
-    order_in, order_out = iota((WIDE, WIDE), 0), iota((WIDE, WIDE), 1)
-    wanted = order_out // dirs % BLOCK * LANES + order_out // (BLOCK * dirs) * dirs + order_out % dirs
-    shuffle = ones_where(order_in == wanted)
-
-    def finish(t, ext):
-        lanes = pl.ds(pl.multiple_of(t * WIDE, WIDE), WIDE)
-        z_real = dot(matrix[...], x_all[0, :, lanes])
-        z_imag = dot(matrix[...], x_all[1, :, lanes])
-        y_real = z_real[:modes] - z_imag[modes:]
-        y_imag = z_real[modes:] + z_imag[:modes]
+    def multiply(t):
+        lanes = slice(t * WIDE, (t + 1) * WIDE)
+        for k in range(2):
+            z_buf[t % 2, k] = dot(matrix[...].reshape(both, classes * modes), x_all[k, :, lanes])
+
+    def fold(t, ext):
+        lanes = slice(t * WIDE, (t + 1) * WIDE)
+        real_real, imag_real = halves(z_buf[t % 2, 0])
+        real_imag, imag_imag = halves(z_buf[t % 2, 1])
+        y_real = real_real - imag_imag
+        y_imag = imag_real + real_imag
         m_real, m_imag = mie_wide[:modes, lanes], mie_wide[modes:, lanes]
         o_real = base[:modes, lanes] + (m_real * y_real - m_imag * y_imag)
         o_imag = base[modes:, lanes] + (m_real * y_imag + m_imag * y_real)
+        out_ref[:modes, lanes] = o_real.astype(BF16)
+        out_ref[modes:, lanes] = o_imag.astype(BF16)
         term = inc[:modes, lanes] * o_real + inc[modes:, lanes] * o_imag
-        out_ref[:modes, lanes] = dot(o_real.astype(BF16), shuffle).astype(BF16)
-        out_ref[modes:, lanes] = dot(o_imag.astype(BF16), shuffle).astype(BF16)
         return ext + term.reshape(modes // 8, 8, WIDE).sum(0)
 
-    ext = lax.fori_loop(0, tiles, finish, jnp.zeros((8, WIDE), F32))
+    ext = jnp.zeros((8, WIDE), F32)
+    multiply(0)
+    for t in range(1, tiles):
+        multiply(t)
+        ext = fold(t - 1, ext)
+    ext = fold(tiles - 1, ext)
     local = (ext[:, :LANES] + ext[:, LANES:]).sum(0, keepdims=True)
     ext_send[...] = local
     ext_recv[me] = local
@@ -296,8 +341,20 @@
         return carry
 
     lax.fori_loop(0, devices - 1, start_ext, 0)
+    store = pltpu.make_async_copy(out_ref, out_hbm, out_sem)
+    store.start()
+    store.wait()
     lax.fori_loop(0, devices - 1, end_ext, 0)
-    total = jnp.broadcast_to(ext_recv[...].sum(0), (8, LANES))
+    ext_ref[...] = ext_recv[...].sum(0)
+
+
+def order_kernel(mixed_ref, lanes_ref, out_ref, ext_ref):
+    dirs = ext_ref.shape[1]
+    order_in, order_out = iota((WIDE, WIDE), 0), iota((WIDE, WIDE), 1)
+    wanted = order_out // dirs % BLOCK * LANES + order_out // (BLOCK * dirs) * dirs + order_out % dirs
+    shuffle = ones_where(order_in == wanted)
+    out_ref[...] = dot(mixed_ref[...], shuffle).astype(BF16)
+    total = jnp.broadcast_to(lanes_ref[...], (8, LANES))
     shift = LANES // 2
     while shift >= dirs:
         total = total + pltpu.roll(total, shift, 1)
@@ -321,16 +378,27 @@
     share = 4 * units // groups
     slots = 2 * devices
     vmem = pl.BlockSpec(memory_space=pltpu.VMEM)
+    anywhere = pl.BlockSpec(memory_space=pl.ANY)
     dma = pltpu.SemaphoreType.DMA
-    scattered, extinction = pl.pallas_call(
+    mixed, lane_sums = pl.pallas_call(
         body,
         out_shape=(
             jax.ShapeDtypeStruct((both, columns), BF16),
-            jax.ShapeDtypeStruct((1, dirs), F32),
+            jax.ShapeDtypeStruct((1, LANES), F32),
         ),
-        in_specs=[vmem] * 9 + [pl.BlockSpec(memory_space=pl.ANY)],
-        out_specs=(vmem, vmem),
+        in_specs=[anywhere] * 10,
+        out_specs=(anywhere, vmem),
         scratch_shapes=[
+            *[pltpu.VMEM((1, pairs), jnp.int32)] * 4,
+            pltpu.VMEM((3, spheres), F32),
+            pltpu.VMEM((3, wave_vectors.shape[0]), F32),
+            pltpu.VMEM((1, dirs), jnp.int32),
+            pltpu.VMEM((2, spheres, modes), F32),
+            pltpu.VMEM((both, wave_vectors.shape[0]), F32),
+            dma((9,)),
+            pltpu.VMEM((both, columns), BF16),
+            dma,
+            pltpu.VMEM((2, 2, both, WIDE), F32),
             pltpu.VMEM((max(1, units // share), devices, share, LANES), BF16),
             pltpu.VMEM((groups, devices, share, LANES), BF16),
             pltpu.VMEM((1, LANES), F32),
@@ -339,8 +407,8 @@
             dma,
             dma((devices,)),
             dma((devices,)),
-            dma((groups,)),
-            dma((groups,)),
+            dma((4, groups)),
+            dma((4, groups)),
             dma((devices,)),
             dma((devices,)),
             pltpu.VMEM((LANES, spheres), F32),
@@ -349,9 +417,9 @@
             pltpu.VMEM((both, columns), F32),
             pltpu.VMEM((both, columns), F32),
             pltpu.VMEM((both, columns), F32),
-            pltpu.VMEM((2, both, 2 * slots), BF16),
+            pltpu.VMEM((2, modes // ROWS, 2, ROWS, 2 * slots), BF16),
             pltpu.VMEM((2, 2 * slots, columns // 2), BF16),
-            pltpu.VMEM((both, classes * modes), BF16),
+            pltpu.VMEM((modes // ROWS, 2, ROWS, classes * modes), BF16),
             pltpu.VMEM((2, classes * modes, columns), BF16),
         ],
         compiler_params=pltpu.CompilerParams(
@@ -370,6 +438,18 @@
         pattern.reshape(both, -1),
         trans_table.reshape(classes, both, modes),
     )
+    block = pl.BlockSpec((both, WIDE), lambda t: (0, t))
+    scattered, extinction = pl.pallas_call(
+        order_kernel,
+        out_shape=(
+            jax.ShapeDtypeStruct((both, columns), BF16),
+            jax.ShapeDtypeStruct((1, dirs), F32),
+        ),
+        grid=(columns // WIDE,),
+        in_specs=[block, pl.BlockSpec((1, LANES), lambda t: (0, 0))],
+        out_specs=(block, pl.BlockSpec((1, dirs), lambda t: (0, 0))),
+        name="order",
+    )(mixed, lane_sums)
     return (scattered, extinction[0])
 
 

time: 105 us -> 99.1 us (0.944)
  local copies, waits for them, and re-layouts: 3.39 us -> 0 us
  Pallas kernels: 101 us -> 98.3 us
    pallas_call x1, Pallas kernels: 101 us -> 94.1 us  [shards(): pl.pallas_call(body, out_shape=(jax.ShapeDtypeStruct((both, columns), BF1...]
    pallas_call x0 -> x1, Pallas kernels: none -> 4.21 us  [shards(): pl.pallas_call(order_kernel, out_shape=(jax.ShapeDtypeStruct((both, colum...]
    unnamed x4 -> x0, local copies, waits for them, and re-layouts: 3.39 us -> none
where the time goes in v3:
time: 99.1 us; the launch traced here: 99 us
  Pallas kernels  98.3 us (99%)
    pallas_call x1, Pallas kernels, shards(): pl.pallas_call(body, out_shape=(jax.ShapeDtypeStruct((both, columns), BF1...  94.1 us
    pallas_call x1, Pallas kernels, shards(): pl.pallas_call(order_kernel, out_shape=(jax.ShapeDtypeStruct((both, colum...  4.21 us

profile of v3, /device:TPU:37, one launch (start us, length us, event | category | flops | bytes accessed | tf_op | source)
XLA Modules:
  0.0 99.0 jit_solution(3448111920070626319)
XLA Ops:
  0.6 94.1 %cluster.1 = (bf16[896,1024]{1,0:T(8,128)(2,1)}, f32[1,128]{1,0:T(1,128)}) custom-call(s32[1,64]{1,0:T(1,128)} %bitcast.16, s32[1,64]{1,0:T(1,128)} %bitcast.17, s32[1,64]{1,0:T(1,128)} %bitcast.18, s32[1,64]{1,0:T(1,128)} %bitcast.19, f32[3,32]{1,0:T(4,128)} %bitcast.15, f32[3,256]{1,0:T(4,128)} %bitcast.14, s32[1,32]{1,0:T(1,128)} %bitcast.20, ...), custom_call_target="tpu_custom_call" | custom-call | tf_op jit(solution)/shard_map/cluster/pallas_call | solution.py:383
  94.7 4.2 %order.1 = (bf16[896,1024]{1,0:T(8,128)(2,1)}, f32[1,32]{1,0:T(1,128)}) custom-call(bf16[896,1024]{1,0:T(8,128)(2,1)} %get-tuple-element.6.mixed_ref, f32[1,128]{1,0:T(1,128)} %get-tuple-element.7.lanes_ref), custom_call_target="tpu_custom_call" | custom-call | tf_op jit(solution)/shard_map/order/pallas_call | solution.py:442

commit v4 on v3

--- a/solution.py
+++ b/solution.py
@@ -55,7 +55,7 @@
     route_hbm, source_hbm, target_hbm, class_hbm, pos_hbm, wave_hbm, dirs_hbm, mie_hbm, pattern_hbm, table_hbm,
     out_hbm, ext_ref,
     route_ref, source_ref, target_ref, class_ref, pos_ref, wave_ref, dirs_ref, mie_ref, pattern_ref, load_sem,
-    out_ref, out_sem, z_buf,
+    out_ref, ordered, out_sem, z_buf,
     send, recv, ext_send, ext_recv, table, table_sem, send_sem, recv_sem, gsend_sem, grecv_sem, esend_sem, erecv_sem,
     parts, mie_rows, pat, mie_wide, inc, base, left, weights, matrix, x_all,
 ):
@@ -79,19 +79,34 @@
 
     barrier = pltpu.get_barrier_semaphore()
 
-    def offset_of(i):
-        return devices // 2 + (i + 1) // 2 * (1 - 2 * lax.rem(i, 2))
-
-    def greet(i, carry):
-        to = lax.rem(me + offset_of(i), devices)
+    middle = devices // 2
+    stride = 5
+
+    def each_peer(act):
+        def pair(e):
+            for number, offset in ((2 * e, middle - e), (2 * e + 1, middle + 1 + e)):
+                to = me + offset
+                act(number, jnp.where(to >= devices, to - devices, to))
+
+        def some(j, carry):
+            for u in range(stride):
+                pair(j * stride + u)
+            return carry
+
+        lax.fori_loop(0, (middle - 1) // stride, some, 0)
+        for e in range((middle - 1) // stride * stride, middle - 1):
+            pair(e)
+        to = me + 1
+        act(devices - 2, jnp.where(to >= devices, to - devices, to))
+
+    def greet(number, to):
         pl.semaphore_signal(barrier, inc=1, device_id={"sph": to}, device_id_type=MESH)
-        return carry
 
     def greet_group(i, carry):
         pl.semaphore_signal(barrier, inc=1, device_id={"groups": lax.rem(group + i, groups)}, device_id_type=MESH)
         return carry
 
-    lax.fori_loop(0, devices - 1, greet, 0)
+    each_peer(greet)
     lax.fori_loop(1, groups, greet_group, 0)
     given = (route_hbm, source_hbm, target_hbm, class_hbm, pos_hbm, mie_hbm, wave_hbm, dirs_hbm, pattern_hbm)
     taken = (route_ref, source_ref, target_ref, class_ref, pos_ref, mie_ref, wave_ref, dirs_ref, pattern_ref)
@@ -138,26 +153,22 @@
 
     pl.semaphore_wait(barrier, devices + groups - 2)
 
-    def exchange(src, dst, sends, receives, offset):
+    def exchange(src, dst, sends, receives, number, to):
         return pltpu.make_async_remote_copy(
             src_ref=src,
             dst_ref=dst,
-            send_sem=sends.at[offset],
-            recv_sem=receives.at[offset],
-            device_id={"sph": lax.rem(me + offset, devices)},
+            send_sem=sends.at[number],
+            recv_sem=receives.at[number],
+            device_id={"sph": to},
             device_id_type=MESH,
         )
 
-    def slot_copy(i):
-        offset = offset_of(i)
-        to = lax.rem(me + offset, devices)
-        return exchange(send.at[piece, to], recv.at[group, i], send_sem, recv_sem, offset)
-
-    def start_slot(i, carry):
-        slot_copy(i).start()
-        return carry
-
-    lax.fori_loop(0, devices - 1, start_slot, 0)
+    neighbour = jnp.where(me + 1 >= devices, 0, me + 1)
+
+    def slot_copy(number, to):
+        return exchange(send.at[piece, to], recv.at[group, number], send_sem, recv_sem, number, to)
+
+    each_peer(lambda number, to: slot_copy(number, to).start())
     recv[group, devices - 1] = send[piece, me]
     for load in loads[6:]:
         load.wait()
@@ -197,7 +208,7 @@
             matrix[:, k, :, c * both : (c + 1) * both] = part
 
     def end_slot(i, carry):
-        copy = slot_copy(i)
+        copy = slot_copy(i, neighbour)
         copy.wait_send()
         copy.wait_recv()
         return carry
@@ -216,14 +227,14 @@
             device_id_type=MESH,
         )
 
-    def start_share(q, carry):
-        lax.fori_loop(q * quarter, jnp.minimum((q + 1) * quarter, devices - 1), end_slot, 0)
+    def start_share(q):
+        lax.fori_loop(q * quarter, min((q + 1) * quarter, devices - 1), end_slot, 0)
 
         def start_one(i, carry):
             share_copy(q, i, False).start()
             return carry
 
-        return lax.fori_loop(1, groups, start_one, carry)
+        lax.fori_loop(1, groups, start_one, 0)
 
     def end_share(q, carry):
         def end_one(i, carry):
@@ -234,7 +245,8 @@
 
         return lax.fori_loop(1, groups, end_one, carry)
 
-    lax.fori_loop(0, 4, start_share, 0)
+    for q in (3, 0, 2, 1):
+        start_share(q)
     lax.fori_loop(0, 4, end_share, 0)
 
     def arrived(s, u):
@@ -323,43 +335,57 @@
     ext = fold(tiles - 1, ext)
     local = (ext[:, :LANES] + ext[:, LANES:]).sum(0, keepdims=True)
     ext_send[...] = local
-    ext_recv[me] = local
-
-    def ext_copy(i, landing):
-        offset = offset_of(i)
-        here = lax.rem(me + devices - offset, devices) if landing else me
-        return exchange(ext_send, ext_recv.at[here], esend_sem, erecv_sem, offset)
-
-    def start_ext(i, carry):
-        ext_copy(i, False).start()
-        return carry
+    ext_recv[devices - 1] = local
+
+    def ext_copy(number, to, here):
+        return exchange(ext_send, ext_recv.at[here], esend_sem, erecv_sem, number, to)
+
+    each_peer(lambda number, to: ext_copy(number, to, number).start())
+
+    order_in, order_out = iota((WIDE, WIDE), 0), iota((WIDE, WIDE), 1)
+    wanted = order_out // dirs % BLOCK * LANES + order_out // (BLOCK * dirs) * dirs + order_out % dirs
+    shuffle = ones_where(order_in == wanted)
+    stores = []
+    for t in range(tiles):
+        lanes = slice(t * WIDE, (t + 1) * WIDE)
+        ordered[t] = dot(out_ref[:, lanes], shuffle).astype(BF16)
+    for t in range(tiles):
+        lanes = slice(t * WIDE, (t + 1) * WIDE)
+        stores.append(pltpu.make_async_copy(ordered.at[t], out_hbm.at[:, lanes], out_sem.at[t]))
+        stores[-1].start()
+    for store in stores:
+        store.wait()
 
     def end_ext(i, carry):
-        copy = ext_copy(i, True)
+        copy = ext_copy(i, neighbour, i)
         copy.wait_send()
         copy.wait_recv()
         return carry
 
-    lax.fori_loop(0, devices - 1, start_ext, 0)
-    store = pltpu.make_async_copy(out_ref, out_hbm, out_sem)
-    store.start()
-    store.wait()
     lax.fori_loop(0, devices - 1, end_ext, 0)
-    ext_ref[...] = ext_recv[...].sum(0)
-
-
-def order_kernel(mixed_ref, lanes_ref, out_ref, ext_ref):
-    dirs = ext_ref.shape[1]
-    order_in, order_out = iota((WIDE, WIDE), 0), iota((WIDE, WIDE), 1)
-    wanted = order_out // dirs % BLOCK * LANES + order_out // (BLOCK * dirs) * dirs + order_out % dirs
-    shuffle = ones_where(order_in == wanted)
-    out_ref[...] = dot(mixed_ref[...], shuffle).astype(BF16)
-    total = jnp.broadcast_to(lanes_ref[...], (8, LANES))
+    total = jnp.broadcast_to(ext_recv[...].sum(0), (8, LANES))
     shift = LANES // 2
     while shift >= dirs:
         total = total + pltpu.roll(total, shift, 1)
         shift //= 2
-    ext_ref[...] = total[0:1, 0:dirs]
+    ext_ref[...] = total[0:1]
+
+
+def hand_over(from_hbm, sums_ref, to_hbm, ext_ref, held, in_sem, out_sem):
+    count = held.shape[0]
+    rows = held.shape[1]
+    takes, gives = [], []
+    for i in range(count):
+        at = slice(i * rows, (i + 1) * rows)
+        takes.append(pltpu.make_async_copy(from_hbm.at[at], held.at[i], in_sem.at[i]))
+        gives.append(pltpu.make_async_copy(held.at[i], to_hbm.at[at], out_sem.at[i]))
+        takes[i].start()
+    ext_ref[...] = sums_ref[0:1, 0 : ext_ref.shape[1]]
+    for i in range(count):
+        takes[i].wait()
+        gives[i].start()
+    for i in range(count):
+        gives[i].wait()
 
 
 def shards(
@@ -397,7 +423,8 @@
             pltpu.VMEM((both, wave_vectors.shape[0]), F32),
             dma((9,)),
             pltpu.VMEM((both, columns), BF16),
-            dma,
+            pltpu.VMEM((columns // WIDE, both, WIDE), BF16),
+            dma((columns // WIDE,)),
             pltpu.VMEM((2, 2, both, WIDE), F32),
             pltpu.VMEM((max(1, units // share), devices, share, LANES), BF16),
             pltpu.VMEM((groups, devices, share, LANES), BF16),
@@ -438,17 +465,22 @@
         pattern.reshape(both, -1),
         trans_table.reshape(classes, both, modes),
     )
-    block = pl.BlockSpec((both, WIDE), lambda t: (0, t))
+    pieces = 8
     scattered, extinction = pl.pallas_call(
-        order_kernel,
+        hand_over,
         out_shape=(
             jax.ShapeDtypeStruct((both, columns), BF16),
             jax.ShapeDtypeStruct((1, dirs), F32),
         ),
-        grid=(columns // WIDE,),
-        in_specs=[block, pl.BlockSpec((1, LANES), lambda t: (0, 0))],
-        out_specs=(block, pl.BlockSpec((1, dirs), lambda t: (0, 0))),
-        name="order",
+        in_specs=[anywhere, vmem],
+        out_specs=(anywhere, vmem),
+        scratch_shapes=[
+            pltpu.VMEM((pieces, both // pieces, columns), BF16),
+            dma((pieces,)),
+            dma((pieces,)),
+        ],
+        compiler_params=pltpu.CompilerParams(vmem_limit_bytes=63 * 1024 * 1024),
+        name="hand_over",
     )(mixed, lane_sums)
     return (scattered, extinction[0])
 

time: 99.1 us -> 96.7 us (0.976)
  Pallas kernels: 98.3 us -> 95.7 us
    pallas_call x1, Pallas kernels: 94.1 us -> 92.1 us  [shards(): pl.pallas_call(body, out_shape=(jax.ShapeDtypeStruct((both, columns), BF1...]
where the time goes in v4:
time: 96.7 us; the launch traced here: 96.5 us
  Pallas kernels  95.7 us (99%)
    pallas_call x1, Pallas kernels, shards(): pl.pallas_call(body, out_shape=(jax.ShapeDtypeStruct((both, columns), BF1...  92.1 us
    pallas_call x1, Pallas kernels, shards(): pl.pallas_call(hand_over, out_shape=(jax.ShapeDtypeStruct((both, columns)...  3.6 us

profile of v4, /device:TPU:37, one launch (start us, length us, event | category | flops | bytes accessed | tf_op | source)
XLA Modules:
  0.0 96.5 jit_solution(4966399947616387048)
XLA Ops:
  0.6 92.1 %cluster.1 = (bf16[896,1024]{1,0:T(8,128)(2,1)}, f32[1,128]{1,0:T(1,128)}) custom-call(s32[1,64]{1,0:T(1,128)} %bitcast.16, s32[1,64]{1,0:T(1,128)} %bitcast.17, s32[1,64]{1,0:T(1,128)} %bitcast.18, s32[1,64]{1,0:T(1,128)} %bitcast.19, f32[3,32]{1,0:T(4,128)} %bitcast.15, f32[3,256]{1,0:T(4,128)} %bitcast.14, s32[1,32]{1,0:T(1,128)} %bitcast.20, ...), custom_call_target="tpu_custom_call" | custom-call | tf_op jit(solution)/shard_map/cluster/pallas_call | solution.py:409
  92.8 3.6 %hand_over.1 = (bf16[896,1024]{1,0:T(8,128)(2,1)}, f32[1,32]{1,0:T(1,128)}) custom-call(bf16[896,1024]{1,0:T(8,128)(2,1)} %get-tuple-element.6.from_hbm, f32[1,128]{1,0:T(1,128)} %get-tuple-element.7.sums_ref), custom_call_target="tpu_custom_call" | custom-call | tf_op jit(solution)/shard_map/hand_over/pallas_call | solution.py:469

commit v5 on v4

--- a/solution.py
+++ b/solution.py
@@ -74,7 +74,8 @@
     tiles = blocks // tile_blocks
     slots = 2 * devices
     units = both // LANES + 1
-    share = recv.shape[2]
+    halvings, bit = recv.shape[0], recv.shape[3]
+    share = halvings * bit
     whole = modes // LANES
 
     barrier = pltpu.get_barrier_semaphore()
@@ -148,7 +149,7 @@
                 rows = mixed if c == 2 else mie_ref[c, :, t * LANES : (t + 1) * LANES]
                 value = dot(pick, rows.astype(BF16))
             at = n * units + u
-            send[at // share, :, at % share, :] = value.astype(BF16)
+            send[at % share // bit, at // share, :, at % bit, :] = value.astype(BF16)
     piece = lax.rem(first_unit, units) // share if share < units else 0
 
     pl.semaphore_wait(barrier, devices + groups - 2)
@@ -165,11 +166,12 @@
 
     neighbour = jnp.where(me + 1 >= devices, 0, me + 1)
 
-    def slot_copy(number, to):
-        return exchange(send.at[piece, to], recv.at[group, number], send_sem, recv_sem, number, to)
-
-    each_peer(lambda number, to: slot_copy(number, to).start())
-    recv[group, devices - 1] = send[piece, me]
+    def slot_copy(h, number, to):
+        return exchange(send.at[h, piece, to], recv.at[h, group, number], send_sem.at[h], recv_sem.at[h], number, to)
+
+    for h in range(halvings):
+        each_peer(lambda number, to: slot_copy(h, number, to).start())
+        recv[h, group, devices - 1] = send[h, piece, me]
     for load in loads[6:]:
         load.wait()
 
@@ -207,53 +209,50 @@
             part = two[k * modes : (k + 1) * modes].reshape(modes // ROWS, ROWS, both)
             matrix[:, k, :, c * both : (c + 1) * both] = part
 
-    def end_slot(i, carry):
-        copy = slot_copy(i, neighbour)
-        copy.wait_send()
-        copy.wait_recv()
-        return carry
-
-    quarter = devices // 4
-
-    def share_copy(q, i, landing):
+    def share_copy(h, i, landing):
         at = lax.rem(group + groups - i, groups) if landing else group
-        rows = pl.ds(q * quarter, quarter)
         return pltpu.make_async_remote_copy(
-            src_ref=recv.at[group, rows],
-            dst_ref=recv.at[at, rows],
-            send_sem=gsend_sem.at[q, i],
-            recv_sem=grecv_sem.at[q, i],
+            src_ref=recv.at[h, group],
+            dst_ref=recv.at[h, at],
+            send_sem=gsend_sem.at[h, i],
+            recv_sem=grecv_sem.at[h, i],
             device_id={"groups": lax.rem(group + i, groups)},
             device_id_type=MESH,
         )
 
-    def start_share(q):
-        lax.fori_loop(q * quarter, min((q + 1) * quarter, devices - 1), end_slot, 0)
-
-        def start_one(i, carry):
-            share_copy(q, i, False).start()
-            return carry
-
-        lax.fori_loop(1, groups, start_one, 0)
-
-    def end_share(q, carry):
-        def end_one(i, carry):
-            copy = share_copy(q, i, True)
+    def start_share(h):
+        def end_slot(i, carry):
+            copy = slot_copy(h, i, neighbour)
             copy.wait_send()
             copy.wait_recv()
             return carry
 
-        return lax.fori_loop(1, groups, end_one, carry)
-
-    for q in (3, 0, 2, 1):
-        start_share(q)
-    lax.fori_loop(0, 4, end_share, 0)
+        def start_one(i, carry):
+            share_copy(h, i, False).start()
+            return carry
+
+        lax.fori_loop(0, devices - 1, end_slot, 0)
+        lax.fori_loop(1, groups, start_one, 0)
+
+    def end_share(h):
+        def end_one(i, carry):
+            copy = share_copy(h, i, True)
+            copy.wait_send()
+            copy.wait_recv()
+            return carry
+
+        lax.fori_loop(1, groups, end_one, 0)
+
+    for h in range(halvings):
+        start_share(h)
+    for h in range(halvings):
+        end_share(h)
 
     def arrived(s, u):
         both_ranks = []
         for r in range(2):
             at = (2 * r + s) * units + u
-            both_ranks.append(recv[at // share, :, at % share, :].astype(F32))
+            both_ranks.append(recv[at % share // bit, at // share, :, at % bit, :].astype(F32))
         return jnp.concatenate(both_ranks, 0)
 
     phases = []
@@ -284,29 +283,29 @@
     code = jnp.where(target > 0.0, meta[:, CLASS_AT : CLASS_AT + 1] * float(blocks) + target - 1.0, -1.0)
     code = jnp.broadcast_to(code, (slots, LANES))
 
-    def form(c, carry):
-        rows = pl.ds(pl.multiple_of(c * modes, 64), modes)
+    def form(c, n):
+        rows = slice(c * modes, (c + 1) * modes) if isinstance(c, int) else pl.ds(pl.multiple_of(c * modes, 64), modes)
         for s in range(2):
             cosine, sine = phases[s]
-            for t in range(tiles):
-                block_of = (iota((slots, LANES), 1) // dirs + t * tile_blocks + c * blocks).astype(F32)
-                hit = code == block_of
-                lanes = slice(t * LANES, (t + 1) * LANES)
-                weights[s, 0:slots, lanes] = jnp.where(hit, cosine, 0.0).astype(BF16)
-                weights[s, slots : 2 * slots, lanes] = jnp.where(hit, sine, 0.0).astype(BF16)
-        for s in range(2):
-            for n in range(tiles // 2):
-                gathered = dot(left[s].reshape(both, 2 * slots), weights[s, :, n * WIDE : (n + 1) * WIDE])
-                for t in range(2):
-                    lanes = slice(t * LANES, (t + 1) * LANES)
-                    g_real, g_imag = halves(gathered[:, lanes])
-                    p_real, p_imag = pat[:modes, :], pat[modes:, :]
-                    at = (2 * n + t) * WIDE + s * LANES
-                    x_all[0, rows, at : at + LANES] = (g_real * p_real - g_imag * p_imag).astype(BF16)
-                    x_all[1, rows, at : at + LANES] = (g_real * p_imag + g_imag * p_real).astype(BF16)
+            for t in range(2):
+                first = (2 * n + t) * tile_blocks + c * blocks
+                hit = code == (iota((slots, LANES), 1) // dirs + first).astype(F32)
+                lanes = slice((2 * n + t) * LANES, (2 * n + t + 1) * LANES)
+                weights[c, s, 0:slots, lanes] = jnp.where(hit, cosine, 0.0).astype(BF16)
+                weights[c, s, slots : 2 * slots, lanes] = jnp.where(hit, sine, 0.0).astype(BF16)
+            gathered = dot(left[s].reshape(both, 2 * slots), weights[c, s, :, n * WIDE : (n + 1) * WIDE])
+            for t in range(2):
+                g_real, g_imag = halves(gathered[:, t * LANES : (t + 1) * LANES])
+                p_real, p_imag = pat[:modes, :], pat[modes:, :]
+                at = (2 * n + t) * WIDE + s * LANES
+                x_all[0, rows, at : at + LANES] = (g_real * p_real - g_imag * p_imag).astype(BF16)
+                x_all[1, rows, at : at + LANES] = (g_real * p_imag + g_imag * p_real).astype(BF16)
+
+    def form_first(c, carry):
+        form(c, 0)
         return carry
 
-    lax.fori_loop(0, classes, form, 0)
+    lax.fori_loop(0, classes, form_first, 0)
 
     def multiply(t):
         lanes = slice(t * WIDE, (t + 1) * WIDE)
@@ -328,10 +327,14 @@
         return ext + term.reshape(modes // 8, 8, WIDE).sum(0)
 
     ext = jnp.zeros((8, WIDE), F32)
-    multiply(0)
-    for t in range(1, tiles):
+    per_tile = classes // 2
+    for t in range(tiles):
         multiply(t)
-        ext = fold(t - 1, ext)
+        if t < 2:
+            for c in range(t * per_tile, (t + 1) * per_tile):
+                form(c, 1)
+        if t > 0:
+            ext = fold(t - 1, ext)
     ext = fold(tiles - 1, ext)
     local = (ext[:, :LANES] + ext[:, LANES:]).sum(0, keepdims=True)
     ext_send[...] = local
@@ -368,10 +371,10 @@
     while shift >= dirs:
         total = total + pltpu.roll(total, shift, 1)
         shift //= 2
-    ext_ref[...] = total[0:1]
-
-
-def hand_over(from_hbm, sums_ref, to_hbm, ext_ref, held, in_sem, out_sem):
+    ext_ref[...] = total[0:1, 0:dirs]
+
+
+def hand_over(from_hbm, sums_hbm, to_hbm, ext_hbm, held, sums, in_sem, out_sem):
     count = held.shape[0]
     rows = held.shape[1]
     takes, gives = [], []
@@ -379,13 +382,15 @@
         at = slice(i * rows, (i + 1) * rows)
         takes.append(pltpu.make_async_copy(from_hbm.at[at], held.at[i], in_sem.at[i]))
         gives.append(pltpu.make_async_copy(held.at[i], to_hbm.at[at], out_sem.at[i]))
-        takes[i].start()
-    ext_ref[...] = sums_ref[0:1, 0 : ext_ref.shape[1]]
-    for i in range(count):
-        takes[i].wait()
-        gives[i].start()
-    for i in range(count):
-        gives[i].wait()
+    takes.append(pltpu.make_async_copy(sums_hbm, sums, in_sem.at[count]))
+    gives.append(pltpu.make_async_copy(sums, ext_hbm, out_sem.at[count]))
+    for take in takes:
+        take.start()
+    for take, give in zip(takes, gives):
+        take.wait()
+        give.start()
+    for give in gives:
+        give.wait()
 
 
 def shards(
@@ -402,6 +407,7 @@
     columns = spheres * dirs
     units = both // LANES + 1
     share = 4 * units // groups
+    waves = 2 if share % 2 == 0 else 1
     slots = 2 * devices
     vmem = pl.BlockSpec(memory_space=pltpu.VMEM)
     anywhere = pl.BlockSpec(memory_space=pl.ANY)
@@ -410,7 +416,7 @@
         body,
         out_shape=(
             jax.ShapeDtypeStruct((both, columns), BF16),
-            jax.ShapeDtypeStruct((1, LANES), F32),
+            jax.ShapeDtypeStruct((1, dirs), F32),
         ),
         in_specs=[anywhere] * 10,
         out_specs=(anywhere, vmem),
@@ -426,16 +432,16 @@
             pltpu.VMEM((columns // WIDE, both, WIDE), BF16),
             dma((columns // WIDE,)),
             pltpu.VMEM((2, 2, both, WIDE), F32),
-            pltpu.VMEM((max(1, units // share), devices, share, LANES), BF16),
-            pltpu.VMEM((groups, devices, share, LANES), BF16),
+            pltpu.VMEM((waves, max(1, units // share), devices, share // waves, LANES), BF16),
+            pltpu.VMEM((waves, groups, devices, share // waves, LANES), BF16),
             pltpu.VMEM((1, LANES), F32),
             pltpu.VMEM((devices, 1, LANES), F32),
             pltpu.VMEM((classes, both, modes), BF16),
             dma,
-            dma((devices,)),
-            dma((devices,)),
-            dma((4, groups)),
-            dma((4, groups)),
+            dma((waves, devices)),
+            dma((waves, devices)),
+            dma((waves, groups)),
+            dma((waves, groups)),
             dma((devices,)),
             dma((devices,)),
             pltpu.VMEM((LANES, spheres), F32),
@@ -445,7 +451,7 @@
             pltpu.VMEM((both, columns), F32),
             pltpu.VMEM((both, columns), F32),
             pltpu.VMEM((2, modes // ROWS, 2, ROWS, 2 * slots), BF16),
-            pltpu.VMEM((2, 2 * slots, columns // 2), BF16),
+            pltpu.VMEM((classes, 2, 2 * slots, columns // 2), BF16),
             pltpu.VMEM((modes // ROWS, 2, ROWS, classes * modes), BF16),
             pltpu.VMEM((2, classes * modes, columns), BF16),
         ],
@@ -472,12 +478,13 @@
             jax.ShapeDtypeStruct((both, columns), BF16),
             jax.ShapeDtypeStruct((1, dirs), F32),
         ),
-        in_specs=[anywhere, vmem],
-        out_specs=(anywhere, vmem),
+        in_specs=[anywhere, anywhere],
+        out_specs=(anywhere, anywhere),
         scratch_shapes=[
             pltpu.VMEM((pieces, both // pieces, columns), BF16),
-            dma((pieces,)),
-            dma((pieces,)),
+            pltpu.VMEM((1, dirs), F32),
+            dma((pieces + 1,)),
+            dma((pieces + 1,)),
         ],
         compiler_params=pltpu.CompilerParams(vmem_limit_bytes=63 * 1024 * 1024),
         name="hand_over",

time: 96.7 us -> 98.8 us (1.022)
  Pallas kernels: 95.7 us -> 97.8 us
    pallas_call x1, Pallas kernels: 92.1 us -> 95.4 us  [shards(): pl.pallas_call(body, out_shape=(jax.ShapeDtypeStruct((both, columns), BF1...]
    pallas_call x1, Pallas kernels: 3.6 us -> 2.43 us  [shards(): pl.pallas_call(hand_over, out_shape=(jax.ShapeDtypeStruct((both, columns)...]
where the time goes in v5:
time: 98.8 us; the launch traced here: 98.6 us
  Pallas kernels  97.8 us (99%)
    pallas_call x1, Pallas kernels, shards(): pl.pallas_call(body, out_shape=(jax.ShapeDtypeStruct((both, columns), BF1...  95.4 us
    pallas_call x1, Pallas kernels, shards(): pl.pallas_call(hand_over, out_shape=(jax.ShapeDtypeStruct((both, columns)...  2.43 us

profile of v5, /device:TPU:37, one launch (start us, length us, event | category | flops | bytes accessed | tf_op | source)
XLA Modules:
  0.0 98.6 jit_solution(17426583026111276499)
XLA Ops:
  0.6 95.4 %cluster.1 = (bf16[896,1024]{1,0:T(8,128)(2,1)}, f32[1,32]{1,0:T(1,128)}) custom-call(s32[1,64]{1,0:T(1,128)} %bitcast.16, s32[1,64]{1,0:T(1,128)} %bitcast.17, s32[1,64]{1,0:T(1,128)} %bitcast.18, s32[1,64]{1,0:T(1,128)} %bitcast.19, f32[3,32]{1,0:T(4,128)} %bitcast.15, f32[3,256]{1,0:T(4,128)} %bitcast.14, s32[1,32]{1,0:T(1,128)} %bitcast.20, ...), custom_call_target="tpu_custom_call" | custom-call | tf_op jit(solution)/shard_map/cluster/pallas_call | solution.py:415
  96.0 2.4 %hand_over.1 = (bf16[896,1024]{1,0:T(8,128)(2,1)}, f32[1,32]{1,0:T(1,128)}) custom-call(bf16[896,1024]{1,0:T(8,128)(2,1)} %get-tuple-element.6.from_hbm, f32[1,32]{1,0:T(1,128)} %get-tuple-element.7.sums_hbm), custom_call_target="tpu_custom_call" | custom-call | tf_op jit(solution)/shard_map/hand_over/pallas_call | solution.py:475

commit v6 on v5

--- a/solution.py
+++ b/solution.py
@@ -56,7 +56,7 @@
     out_hbm, ext_ref,
     route_ref, source_ref, target_ref, class_ref, pos_ref, wave_ref, dirs_ref, mie_ref, pattern_ref, load_sem,
     out_ref, ordered, out_sem, z_buf,
-    send, recv, ext_send, ext_recv, table, table_sem, send_sem, recv_sem, gsend_sem, grecv_sem, esend_sem, erecv_sem,
+    send, recv, ext_send, ext_mid, near_recv, ext_recv, table, table_sem, send_sem, recv_sem, gsend_sem, grecv_sem, esend_sem, erecv_sem,
     parts, mie_rows, pat, mie_wide, inc, base, left, weights, matrix, x_all,
 ):
     me = lax.axis_index("sph")
@@ -74,8 +74,7 @@
     tiles = blocks // tile_blocks
     slots = 2 * devices
     units = both // LANES + 1
-    halvings, bit = recv.shape[0], recv.shape[3]
-    share = halvings * bit
+    share = recv.shape[2]
     whole = modes // LANES
 
     barrier = pltpu.get_barrier_semaphore()
@@ -149,7 +148,7 @@
                 rows = mixed if c == 2 else mie_ref[c, :, t * LANES : (t + 1) * LANES]
                 value = dot(pick, rows.astype(BF16))
             at = n * units + u
-            send[at % share // bit, at // share, :, at % bit, :] = value.astype(BF16)
+            send[at // share, :, at % share, :] = value.astype(BF16)
     piece = lax.rem(first_unit, units) // share if share < units else 0
 
     pl.semaphore_wait(barrier, devices + groups - 2)
@@ -166,12 +165,11 @@
 
     neighbour = jnp.where(me + 1 >= devices, 0, me + 1)
 
-    def slot_copy(h, number, to):
-        return exchange(send.at[h, piece, to], recv.at[h, group, number], send_sem.at[h], recv_sem.at[h], number, to)
-
-    for h in range(halvings):
-        each_peer(lambda number, to: slot_copy(h, number, to).start())
-        recv[h, group, devices - 1] = send[h, piece, me]
+    def slot_copy(number, to):
+        return exchange(send.at[piece, to], recv.at[group, number], send_sem, recv_sem, number, to)
+
+    each_peer(lambda number, to: slot_copy(number, to).start())
+    recv[group, devices - 1] = send[piece, me]
     for load in loads[6:]:
         load.wait()
 
@@ -209,50 +207,53 @@
             part = two[k * modes : (k + 1) * modes].reshape(modes // ROWS, ROWS, both)
             matrix[:, k, :, c * both : (c + 1) * both] = part
 
-    def share_copy(h, i, landing):
+    def end_slot(i, carry):
+        copy = slot_copy(i, neighbour)
+        copy.wait_send()
+        copy.wait_recv()
+        return carry
+
+    quarter = devices // 4
+
+    def share_copy(q, i, landing):
         at = lax.rem(group + groups - i, groups) if landing else group
+        rows = pl.ds(q * quarter, quarter)
         return pltpu.make_async_remote_copy(
-            src_ref=recv.at[h, group],
-            dst_ref=recv.at[h, at],
-            send_sem=gsend_sem.at[h, i],
-            recv_sem=grecv_sem.at[h, i],
+            src_ref=recv.at[group, rows],
+            dst_ref=recv.at[at, rows],
+            send_sem=gsend_sem.at[q, i],
+            recv_sem=grecv_sem.at[q, i],
             device_id={"groups": lax.rem(group + i, groups)},
             device_id_type=MESH,
         )
 
-    def start_share(h):
-        def end_slot(i, carry):
-            copy = slot_copy(h, i, neighbour)
+    def start_share(q):
+        lax.fori_loop(q * quarter, min((q + 1) * quarter, devices - 1), end_slot, 0)
+
+        def start_one(i, carry):
+            share_copy(q, i, False).start()
+            return carry
+
+        lax.fori_loop(1, groups, start_one, 0)
+
+    def end_share(q, carry):
+        def end_one(i, carry):
+            copy = share_copy(q, i, True)
             copy.wait_send()
             copy.wait_recv()
             return carry
 
-        def start_one(i, carry):
-            share_copy(h, i, False).start()
-            return carry
-
-        lax.fori_loop(0, devices - 1, end_slot, 0)
-        lax.fori_loop(1, groups, start_one, 0)
-
-    def end_share(h):
-        def end_one(i, carry):
-            copy = share_copy(h, i, True)
-            copy.wait_send()
-            copy.wait_recv()
-            return carry
-
-        lax.fori_loop(1, groups, end_one, 0)
-
-    for h in range(halvings):
-        start_share(h)
-    for h in range(halvings):
-        end_share(h)
+        return lax.fori_loop(1, groups, end_one, carry)
+
+    for q in (3, 0, 2, 1):
+        start_share(q)
+    lax.fori_loop(0, 4, end_share, 0)
 
     def arrived(s, u):
         both_ranks = []
         for r in range(2):
             at = (2 * r + s) * units + u
-            both_ranks.append(recv[at % share // bit, at // share, :, at % bit, :].astype(F32))
+            both_ranks.append(recv[at // share, :, at % share, :].astype(F32))
         return jnp.concatenate(both_ranks, 0)
 
     phases = []
@@ -337,13 +338,30 @@
             ext = fold(t - 1, ext)
     ext = fold(tiles - 1, ext)
     local = (ext[:, :LANES] + ext[:, LANES:]).sum(0, keepdims=True)
+    near, far = near_recv.shape[0], ext_recv.shape[0]
+    first = me // near * near
+
+    def near_copy(i):
+        return exchange(ext_send, near_recv.at[i], esend_sem, erecv_sem, i, first + lax.rem(me + i, near))
+
+    def far_copy(i):
+        to = me + near * i
+        to = jnp.where(to >= devices, to - devices, to)
+        return exchange(ext_mid, ext_recv.at[i], esend_sem, erecv_sem, near + i, to)
+
     ext_send[...] = local
-    ext_recv[devices - 1] = local
-
-    def ext_copy(number, to, here):
-        return exchange(ext_send, ext_recv.at[here], esend_sem, erecv_sem, number, to)
-
-    each_peer(lambda number, to: ext_copy(number, to, number).start())
+    near_recv[0] = local
+    for i in range(1, near):
+        near_copy(i).start()
+    for i in range(1, near):
+        copy = near_copy(i)
+        copy.wait_send()
+        copy.wait_recv()
+    gathered = near_recv[...].sum(0)
+    ext_mid[...] = gathered
+    ext_recv[0] = gathered
+    for i in sorted(range(1, far), key=lambda i: abs(i - far // 2)):
+        far_copy(i).start()
 
     order_in, order_out = iota((WIDE, WIDE), 0), iota((WIDE, WIDE), 1)
     wanted = order_out // dirs % BLOCK * LANES + order_out // (BLOCK * dirs) * dirs + order_out % dirs
@@ -359,13 +377,10 @@
     for store in stores:
         store.wait()
 
-    def end_ext(i, carry):
-        copy = ext_copy(i, neighbour, i)
+    for i in range(1, far):
+        copy = far_copy(i)
         copy.wait_send()
         copy.wait_recv()
-        return carry
-
-    lax.fori_loop(0, devices - 1, end_ext, 0)
     total = jnp.broadcast_to(ext_recv[...].sum(0), (8, LANES))
     shift = LANES // 2
     while shift >= dirs:
@@ -407,8 +422,8 @@
     columns = spheres * dirs
     units = both // LANES + 1
     share = 4 * units // groups
-    waves = 2 if share % 2 == 0 else 1
     slots = 2 * devices
+    near = 4
     vmem = pl.BlockSpec(memory_space=pltpu.VMEM)
     anywhere = pl.BlockSpec(memory_space=pl.ANY)
     dma = pltpu.SemaphoreType.DMA
@@ -432,16 +447,18 @@
             pltpu.VMEM((columns // WIDE, both, WIDE), BF16),
             dma((columns // WIDE,)),
             pltpu.VMEM((2, 2, both, WIDE), F32),
-            pltpu.VMEM((waves, max(1, units // share), devices, share // waves, LANES), BF16),
-            pltpu.VMEM((waves, groups, devices, share // waves, LANES), BF16),
+            pltpu.VMEM((max(1, units // share), devices, share, LANES), BF16),
+            pltpu.VMEM((groups, devices, share, LANES), BF16),
             pltpu.VMEM((1, LANES), F32),
-            pltpu.VMEM((devices, 1, LANES), F32),
+            pltpu.VMEM((1, LANES), F32),
+            pltpu.VMEM((near, 1, LANES), F32),
+            pltpu.VMEM((devices // near, 1, LANES), F32),
             pltpu.VMEM((classes, both, modes), BF16),
             dma,
-            dma((waves, devices)),
-            dma((waves, devices)),
-            dma((waves, groups)),
-            dma((waves, groups)),
+            dma((devices,)),
+            dma((devices,)),
+            dma((4, groups)),
+            dma((4, groups)),
             dma((devices,)),
             dma((devices,)),
             pltpu.VMEM((LANES, spheres), F32),

time: 98.8 us -> 96.5 us (0.977)
  Pallas kernels: 97.8 us -> 95.6 us
    pallas_call x1, Pallas kernels: 95.4 us -> 93.2 us  [shards(): pl.pallas_call(body, out_shape=(jax.ShapeDtypeStruct((both, columns), BF1...]
where the time goes in v6:
time: 96.5 us; the launch traced here: 96.4 us
  Pallas kernels  95.6 us (99%)
    pallas_call x1, Pallas kernels, shards(): pl.pallas_call(body, out_shape=(jax.ShapeDtypeStruct((both, columns), BF1...  93.2 us
    pallas_call x1, Pallas kernels, shards(): pl.pallas_call(hand_over, out_shape=(jax.ShapeDtypeStruct((both, columns)...  2.43 us

profile of v6, /device:TPU:37, one launch (start us, length us, event | category | flops | bytes accessed | tf_op | source)
XLA Modules:
  0.0 96.4 jit_solution(2956258575881086438)
XLA Ops:
  0.6 93.2 %cluster.1 = (bf16[896,1024]{1,0:T(8,128)(2,1)}, f32[1,32]{1,0:T(1,128)}) custom-call(s32[1,64]{1,0:T(1,128)} %bitcast.16, s32[1,64]{1,0:T(1,128)} %bitcast.17, s32[1,64]{1,0:T(1,128)} %bitcast.18, s32[1,64]{1,0:T(1,128)} %bitcast.19, f32[3,32]{1,0:T(4,128)} %bitcast.15, f32[3,256]{1,0:T(4,128)} %bitcast.14, s32[1,32]{1,0:T(1,128)} %bitcast.20, ...), custom_call_target="tpu_custom_call" | custom-call | tf_op jit(solution)/shard_map/cluster/pallas_call | solution.py:430
  93.8 2.4 %hand_over.1 = (bf16[896,1024]{1,0:T(8,128)(2,1)}, f32[1,32]{1,0:T(1,128)}) custom-call(bf16[896,1024]{1,0:T(8,128)(2,1)} %get-tuple-element.6.from_hbm, f32[1,32]{1,0:T(1,128)} %get-tuple-element.7.sums_hbm), custom_call_target="tpu_custom_call" | custom-call | tf_op jit(solution)/shard_map/hand_over/pallas_call | solution.py:492
